TPU v7x, 16 devices: a whole 2x2x2 slice. The times are simulated.
16 devices in a mesh: dp: 4 (over z, y), tp: 4 (over x, core).
Axes of the slice: x: 2, y: 2, z: 2, core: 2. Of those that a mesh axis runs over, the one named last changes fastest.
Arguments:
- tok_hidden: bfloat16 [256, 1536], P('dp'), parts along dimension 0
- seq_lens: int32 [256], P('dp'), parts along dimension 0
- k_cache: bfloat16 [256, 512, 4, 128], P('dp', None, 'tp'), parts along dimension 0
- v_cache: bfloat16 [256, 512, 4, 128], P('dp', None, 'tp'), parts along dimension 0
- next_tok: int32 [256], P('dp'), parts along dimension 0
- g_attn: bfloat16 [1536], replicated
- w_q: bfloat16 [1536, 1536], P(None, 'tp')
- b_q: bfloat16 [1536], P('tp')
- w_k: bfloat16 [1536, 512], P(None, 'tp')
- b_k: bfloat16 [512], P('tp')
- w_v: bfloat16 [1536, 512], P(None, 'tp')
- b_v: bfloat16 [512], P('tp')
- w_o: bfloat16 [1536, 1536], P('tp')
- g_mlp: bfloat16 [1536], replicated
- w_gate: bfloat16 [1536, 8960], P(None, 'tp')
- w_up: bfloat16 [1536, 8960], P(None, 'tp')
- w_down: bfloat16 [8960, 1536], P('tp')
- g_final: bfloat16 [1536], replicated
- w_head: bfloat16 [151936, 1536], P('tp')
Outputs:
- output 1: bfloat16 [256, 1536], P('dp'), parts along dimension 0
- output 2: bfloat16 [256, 512, 4, 128], P('dp', None, 'tp'), parts along dimension 0
- output 3: bfloat16 [256, 512, 4, 128], P('dp', None, 'tp'), parts along dimension 0
- output 4: float32 [256], P('dp'), parts along dimension 0
- output 5: float32 [256], P('dp'), parts along dimension 0
There are 4 independent parts. A program takes and returns all parts, laid end to end along the dimension named above; an argument that names none is the same for every part.
All inputs are finite; a program needn't handle non-finite values.
Results may differ from a plain program's by a relative error of at most 0.0126328.
Values are sent between devices in bfloat16 or wider.
A program may use at most 1 GiB of HBM per device.

v0:
```python
import jax
import jax.numpy as jnp
from jax import lax
from jax.sharding import PartitionSpec as P

THETA = 1000000.0
EPS = 1e-6


def rms_norm(values, gain_vec):
    vals_f32 = values.astype(jnp.float32)
    inv_rms = lax.rsqrt(jnp.mean(vals_f32 * vals_f32, axis=-1, keepdims=True) + EPS)
    return (vals_f32 * inv_rms * gain_vec.astype(jnp.float32)).astype(jnp.bfloat16)


def rotary(values, positions):
    half_dim = values.shape[-1] // 2
    inv_freq = jnp.power(THETA, jnp.arange(half_dim, dtype=jnp.float32) * (-2.0 / values.shape[-1]))
    angles = positions.astype(jnp.float32)[:, None] * inv_freq[None, :]
    cos_part = jnp.cos(angles)[:, None, :]
    sin_part = jnp.sin(angles)[:, None, :]
    first_half = values[..., :half_dim]
    second_half = values[..., half_dim:]
    return jnp.concatenate([first_half * cos_part - second_half * sin_part, second_half * cos_part + first_half * sin_part], axis=-1)


def attention_block(tok_hidden, seq_lens, k_cache, v_cache, g_attn, w_q, b_q, w_k, b_k, w_v, b_v):
    num_rows = tok_hidden.shape[0]
    cache_len = k_cache.shape[1]
    slot_count = k_cache.shape[2]
    head_dim = k_cache.shape[3]
    head_count = w_q.shape[1] // head_dim
    group_size = head_count // slot_count
    normed = rms_norm(tok_hidden, g_attn)
    q_proj = jnp.dot(normed, w_q, preferred_element_type=jnp.float32) + b_q.astype(jnp.float32)
    k_proj = jnp.dot(normed, w_k, preferred_element_type=jnp.float32) + b_k.astype(jnp.float32)
    v_proj = jnp.dot(normed, w_v, preferred_element_type=jnp.float32) + b_v.astype(jnp.float32)
    q_rot = rotary(q_proj.reshape(num_rows, head_count, head_dim), seq_lens).astype(jnp.bfloat16)
    k_new = rotary(k_proj.reshape(num_rows, slot_count, head_dim), seq_lens).astype(jnp.bfloat16)
    v_new = v_proj.reshape(num_rows, slot_count, head_dim).astype(jnp.bfloat16)
    slot_ids = lax.broadcasted_iota(jnp.int32, (1, cache_len, 1, 1), 1)
    write_mask = slot_ids == seq_lens[:, None, None, None]
    k_all = jnp.where(write_mask, k_new[:, None], k_cache)
    v_all = jnp.where(write_mask, v_new[:, None], v_cache)
    q_grp = q_rot.reshape(num_rows, slot_count, group_size, head_dim)
    scores = jnp.einsum('bkgd,blkd->bkgl', q_grp, k_all, preferred_element_type=jnp.float32) * (head_dim ** -0.5)
    score_ids = lax.broadcasted_iota(jnp.int32, (1, 1, 1, cache_len), 3)
    scores = jnp.where(score_ids <= seq_lens[:, None, None, None], scores, -jnp.inf)
    row_max = jnp.max(scores, axis=-1, keepdims=True)
    exp_scores = jnp.exp(scores - row_max)
    attn_probs = (exp_scores / jnp.sum(exp_scores, axis=-1, keepdims=True)).astype(jnp.bfloat16)
    attn_vals = jnp.einsum('bkgl,blkd->bkgd', attn_probs, v_all, preferred_element_type=jnp.float32)
    attn_out = attn_vals.astype(jnp.bfloat16).reshape(num_rows, head_count * head_dim)
    return attn_out, k_all, v_all


def local_step(tok_hidden, seq_lens, k_cache, v_cache, next_tok, g_attn, w_q, b_q, w_k, b_k, w_v, b_v, w_o, g_mlp, w_gate, w_up, w_down, g_final, w_head):
    attn_out, k_all, v_all = attention_block(tok_hidden, seq_lens, k_cache, v_cache, g_attn, w_q, b_q, w_k, b_k, w_v, b_v)
    attn_part = jnp.dot(attn_out, w_o, preferred_element_type=jnp.float32).astype(jnp.bfloat16)
    attn_sum = lax.psum(attn_part, 'tp')
    residual = (tok_hidden.astype(jnp.float32) + attn_sum.astype(jnp.float32)).astype(jnp.bfloat16)
    mlp_in = rms_norm(residual, g_mlp)
    gate_proj = jnp.dot(mlp_in, w_gate, preferred_element_type=jnp.float32)
    up_proj = jnp.dot(mlp_in, w_up, preferred_element_type=jnp.float32)
    hidden = (jax.nn.silu(gate_proj) * up_proj).astype(jnp.bfloat16)
    down_part = jnp.dot(hidden, w_down, preferred_element_type=jnp.float32).astype(jnp.bfloat16)
    down_sum = lax.psum(down_part, 'tp')
    y_out = (residual.astype(jnp.float32) + down_sum.astype(jnp.float32)).astype(jnp.bfloat16)
    final_norm = rms_norm(y_out, g_final)
    logits = lax.dot_general(final_norm, w_head, (((1,), (1,)), ((), ())), preferred_element_type=jnp.float32)
    vocab_loc = w_head.shape[0]
    vocab_ids = lax.broadcasted_iota(jnp.int32, (1, vocab_loc), 1)
    local_tok = next_tok - lax.axis_index('tp') * vocab_loc
    local_max = jnp.max(logits, axis=1)
    local_sum = jnp.sum(jnp.exp(logits - local_max[:, None]), axis=1)
    local_target = jnp.sum(jnp.where(vocab_ids == local_tok[:, None], logits, 0.0), axis=1)
    all_stats = lax.all_gather(jnp.stack([local_max, local_sum, local_target]), 'tp')
    glob_max = jnp.max(all_stats[:, 0], axis=0)
    exp_total = jnp.sum(all_stats[:, 1] * jnp.exp(all_stats[:, 0] - glob_max[None, :]), axis=0)
    norm_lse = glob_max + jnp.log(exp_total)
    tok_logp = jnp.sum(all_stats[:, 2], axis=0) - norm_lse
    return y_out, k_all, v_all, tok_logp, norm_lse


def solution(mesh):
    row_spec = P('dp', None)
    vec_spec = P('dp')
    cache_spec = P('dp', None, 'tp', None)
    col_spec = P(None, 'tp')
    part_spec = P('tp')
    whole_spec = P(None)
    in_specs = (row_spec, vec_spec, cache_spec, cache_spec, vec_spec, whole_spec, col_spec, part_spec, col_spec, part_spec, col_spec, part_spec, P('tp', None), whole_spec, col_spec, col_spec, P('tp', None), whole_spec, P('tp', None))
    out_specs = (row_spec, cache_spec, cache_spec, vec_spec, vec_spec)
    return jax.shard_map(local_step, mesh=mesh, in_specs=in_specs, out_specs=out_specs, check_vma=False)
```

profile of v0, /device:TPU:0, one launch (start us, length us, event | category | flops | bytes accessed | tf_op | source)
XLA Modules:
  0.0 184.2 jit_solution(5506231662960583607)
XLA Ops:
  7.2 0.0 copy-start
  7.2 0.0 all-reduce.3.cloned.1.call-start
  7.2 0.7 convert_element_type.89
  8.0 0.8 iota_compare_fusion.2
  8.8 0.7 convert_element_type.86
  9.4 1.1 fusion.27
  10.5 0.7 convert_element_type.90
  11.2 0.2 multiply_cosine_fusion.1
  11.4 1.4 fusion.14
  12.8 0.2 fusion.59
  13.0 0.7 convert_element_type.92
  13.6 0.7 convert_element_type.88
  14.3 1.7 convolution_add_fusion
  16.1 0.1 pad_maximum_fusion
  16.2 1.4 fusion.18
  17.5 0.2 subtract_convert_fusion
  17.7 11.9 %broadcast_select_fusion.1 = (bf16[64,512,1,128]{3,1,2,0:T(8,128)(2,1)}, bf16[64,512,1,128]{3,1,2,0:T(8,128)(2,1)}) fusion(bf16[64,512,1,128]{3,1,2,0:T(8,128)(2,1)} %param.21, pred[64,512]{1,0:T(8,128)(4,1)S(1)} %get-tuple-element.26, bf16[64,128]{1,0:T(8,128)(2,1)S(1)} %pad_maximum_fusion, bf16[64,512,1,128]{3,1,2,0:T(8,128)(2,1)} %param.22, ...), kind=kLoop, calls=%fused_computation.9 | loop fusion | flops 8388608 | bytes 33619968 | tf_op jit(solution)/shard_map/jit(_where)/select_n | solution.py:43
  29.6 0.0 copy-start.4
  29.6 0.0 copy-start.2
  29.6 5.9 %fusion.68 = (f32[64,3]{1,0:T(8,128)S(1)}, f32[64,3,512]{2,1,0:T(4,128)S(1)}) fusion(bf16[64,512,1,128]{3,1,2,0:T(8,128)(2,1)} %get-tuple-element.19, pred[64,512]{1,0:T(8,128)(4,1)S(1)} %get-tuple-element.25, bf16[64,3,64]{2,1,0:T(4,128)(2,1)S(1)} %get-tuple-element.16, bf16[64,3,64]{2,1,0:T(4,128)(2,1)S(1)} %get-tuple-element.15), kind=kOutput, calls=%fused_computation.92 | convolution fusion | flops 25657856 | bytes 8864512 | tf_op jit(solution)/shard_map/sub | solution.py:50
  35.5 4.6 %fusion.11 = bf16[64,3,128]{2,1,0:T(4,128)(2,1)S(1)} fusion(bf16[64,512,1,128]{3,1,2,0:T(8,128)(2,1)} %get-tuple-element.20, f32[64,3,512]{2,1,0:T(4,128)S(1)} %get-tuple-element.28, f32[64,3]{1,0:T(8,128)S(1)} %get-tuple-element.27), kind=kOutput, calls=%fused_computation.18 | convolution fusion | flops 25387008 | bytes 8831744 | tf_op jit(solution)/shard_map/bkgl,blkd->bkgd/dot_general | solution.py:52
  40.1 0.0 copy-done
  40.1 1.0 convolution_convert_fusion.1
  41.2 0.0 all-reduce.3.cloned.1.call-update
  41.2 0.2 all-reduce.5.cloned.1.call-start
  41.4 0.0 copy-done.4
  41.4 30.9 %all-reduce.3.cloned.1.call-done = bf16[64,1536]{1,0:T(8,128)(2,1)} async-done(((bf16[64,1536]{1,0:T(8,128)(2,1)}), bf16[64,1536]{1,0:T(8,128)(2,1)}) %all-reduce.3.cloned.1.call-update) | async-done | bytes 196624 | tf_op jit(solution)/shard_map/psum | solution.py:60
  72.4 0.0 copy-done.2
  72.4 1.1 fusion.31
  73.5 5.2 %fusion.46 = f32[64,2240]{1,0:T(8,128)S(1)} fusion(bf16[1536,2240]{0,1:T(8,128)(2,1)} %param.33, bf16[64,1536]{1,0:T(8,128)(2,1)S(1)} %get-tuple-element.14, f32[1536]{0:T(1024)S(1)} %convert_element_type.99, f32[64]{0:T(128)S(1)} %add_rsqrt_fusion.1), kind=kOutput, calls=%fused_computation.61 | convolution fusion | flops 440795136 | bytes 7657728 | tf_op jit(solution)/shard_map/dot_general | solution.py:63
  78.6 0.0 copy-start.6
  78.7 0.0 copy-start.5
  78.7 9.2 %convolution_convert_fusion = bf16[64,1536]{1,0:T(8,128)(2,1)} fusion(bf16[2240,1536]{1,0:T(8,128)(2,1)} %param.35, bf16[1536,2240]{0,1:T(8,128)(2,1)} %param.34, f32[64,2240]{1,0:T(8,128)S(1)} %fusion.46, bf16[64,1536]{1,0:T(8,128)(2,1)S(1)} %get-tuple-element.14, f32[1536]{0:T(1024)S(1)} %convert_element_type.99, f32[64]{0:T(128)S(1)} %add_rsqrt_fusion.1), kind=kOutput, calls=%fused_computation.12 | convolution fusion | flops 882155520 | bytes 14735616 | tf_op jit(solution)/shard_map/dot_general | solution.py:66
  87.8 0.0 all-reduce.5.cloned.1.call-update
  87.9 0.0 copy-done.6
  87.9 0.0 copy-done.5
  87.9 28.3 %all-reduce.5.cloned.1.call-done = bf16[64,1536]{1,0:T(8,128)(2,1)} async-done(((bf16[64,1536]{1,0:T(8,128)(2,1)}), bf16[64,1536]{1,0:T(8,128)(2,1)}) %all-reduce.5.cloned.1.call-update) | async-done | bytes 196624 | tf_op jit(solution)/shard_map/psum | solution.py:67
  116.2 1.1 fusion.24
  117.3 0.0 copy-start.3
  117.3 0.0 copy-start.1
  117.4 48.0 %fusion.69 = (f32[64]{0:T(128)S(1)}, f32[64,37984]{1,0:T(8,128)}) fusion(bf16[37984,1536]{1,0:T(8,128)(2,1)} %param.37, bf16[64,1536]{1,0:T(8,128)(2,1)S(1)} %get-tuple-element.12, f32[1536]{0:T(1024)S(1)} %convert_element_type.106, f32[64]{0:T(128)S(1)} %add_rsqrt_fusion), kind=kOutput, calls=%fused_computation.93 | convolution fusion | flops 7470782464 | bytes 126614016 | tf_op jit(solution)/shard_map/dot_general | solution.py:70
  165.4 0.0 copy-done.3
  165.4 6.2 %exponential_reduce_fusion = (f32[64]{0:T(128)S(1)}, f32[64]{0:T(128)S(1)}) fusion(f32[64,37984]{1,0:T(8,128)} %get-tuple-element.30, f32[64]{0:T(128)S(1)} %get-tuple-element.29, s32[64]{0:T(128)S(1)} %broadcast_subtract_fusion), kind=kLoop, calls=%fused_computation.3 | loop fusion | flops 12154752 | bytes 9724928 | tf_op jit(solution)/shard_map/reduce_sum | solution.py:75
  171.6 5.2 %all-gather.1 = f32[4,3,64]{2,1,0:T(4,128)S(1)} all-gather(f32[1,3,64]{2,1,0:T(4,128)S(1)} %maximum_bitcast_fusion), channel_id=2, replica_groups=mesh['dp'=4,'tp'=4] {'tp'}, dimensions={0}, use_global_device_ids=true | all-gather | bytes 3840 | tf_op jit(solution)/shard_map/all_gather | solution.py:77
  176.8 0.5 fusion.65
  177.3 0.0 copy-done.1
  (11 shorter events, 0.1 us)
Async XLA Ops:
  7.2 33.0 %copy-start = (bf16[384,1536]{1,0:T(8,128)(2,1)S(1)}, bf16[384,1536]{1,0:T(8,128)(2,1)}, u32[]{:S(2)}) copy-start(bf16[384,1536]{1,0:T(8,128)(2,1)} %param.31) | copy-start | bytes 3538948
  7.2 65.2 %all-reduce.3.cloned.1.call-start = ((), (), s32[]{:S(2)}) async-start(), calls=%async_computation | async-start | bytes 393216 | tf_op jit(solution)/shard_map/psum | solution.py:60
  29.6 11.8 %copy-start.4 = (bf16[1536]{0:T(1024)(128)(2,1)S(1)}, bf16[1536]{0:T(1024)(128)(2,1)}, u32[]{:S(2)}) copy-start(bf16[1536]{0:T(1024)(128)(2,1)} %param.32) | copy-start | bytes 9220
  29.6 42.8 %copy-start.2 = (bf16[64,1536]{1,0:T(8,128)(2,1)S(1)}, bf16[64,1536]{1,0:T(8,128)(2,1)}, u32[]{:S(2)}) copy-start(bf16[64,1536]{1,0:T(8,128)(2,1)} %param.19) | copy-start | bytes 589828
  41.2 75.0 %all-reduce.5.cloned.1.call-start = ((), (), s32[]{:S(2)}) async-start(), calls=%async_computation.1 | async-start | bytes 393216 | tf_op jit(solution)/shard_map/psum | solution.py:67
  78.6 9.2 %copy-start.6 = (s32[64]{0:T(128)S(1)}, s32[64]{0:T(128)}, u32[]{:S(2)}) copy-start(s32[64]{0:T(128)} %param.23) | copy-start | bytes 772
  78.7 9.2 %copy-start.5 = (bf16[1536]{0:T(1024)(128)(2,1)S(1)}, bf16[1536]{0:T(1024)(128)(2,1)}, u32[]{:S(2)}) copy-start(bf16[1536]{0:T(1024)(128)(2,1)} %param.36) | copy-start | bytes 9220
  117.3 48.1 %copy-start.3 = (bf16[64,1536]{1,0:T(8,128)(2,1)}, bf16[64,1536]{1,0:T(8,128)(2,1)S(1)}, u32[]{:S(2)}) copy-start(bf16[64,1536]{1,0:T(8,128)(2,1)S(1)} %get-tuple-element.12) | copy-start | bytes 589828
  117.3 60.0 %copy-start.1 = (bf16[384,1536]{1,0:T(8,128)(2,1)S(1)}, bf16[384,1536]{1,0:T(8,128)(2,1)}, u32[]{:S(2)}) copy-start(bf16[384,1536]{1,0:T(8,128)(2,1)} %param.31) | copy-start | bytes 3538948
Sparse Core Ops, SparseCore 0:
  41.3 31.0 all-reduce.2
  88.0 28.1 all-reduce.4
where the time goes:
time: 185 us; the launch traced here: 184 us
  matrix products  78.4 us (42%)
  waiting for transfers between devices  59.3 us (32%)
  other arithmetic  26.8 us (14%)
  between operations  14.3 us (8%)
  blocking collectives  5.17 us (3%)
    dot_general x1, matrix products, local_step(): lax.dot_general(final_norm, w_head, (((1,), (1,)), ((), ())), preferred_e...  48 us
    psum x1, waiting for transfers between devices, local_step(): attn_sum = lax.psum(attn_part, 'tp')  30.9 us
    psum x1, waiting for transfers between devices, local_step(): down_sum = lax.psum(down_part, 'tp')  28.3 us
    select_n x1, other arithmetic, attention_block(): k_all = jnp.where(write_mask, k_new[:, None], k_cache)  11.9 us
    dot_general x1, matrix products, local_step(): jnp.dot(hidden, w_down, preferred_element_type=jnp.float32)  9.17 us
    reduce_sum x1, other arithmetic, local_step(): local_sum = jnp.sum(jnp.exp(logits - local_max[:, None]), axis=1)  6.17 us
    sub x1, matrix products, attention_block(): exp_scores = jnp.exp(scores - row_max)  5.9 us
    all_gather x1, blocking collectives, local_step(): lax.all_gather(jnp.stack([local_max, local_sum, local_target]), 'tp')  5.17 us
  transfers between devices with their start and end apart: 2, of which 2 were waited for; matrix products, arithmetic and copies ran while one was open for 0% of the time, Pallas kernels for 0%

commit v1 on v0

v1 whole, which is shorter than its diff:
```python
import functools
import math
import jax
import jax.numpy as jnp
import numpy as np
from jax import lax
from jax.experimental import pallas as pl
from jax.experimental.pallas import tpu as pltpu
from jax.sharding import PartitionSpec as P

THETA = 1000000.0
EPS = 1e-6
MESH = pl.DeviceIdType.MESH
F32 = jnp.float32
BF16 = jnp.bfloat16

B = 64
L = 512
D = 1536
HD = 128
G = 3
FF = 2240
VOC = 37984
NDP = 4
NTP = 4
NB = 8
NCH = B // NB
VQ = VOC // NDP
VC = 528
NVC = 18
HALF = B // 2
FF_CHUNKS = ((0, 512), (512, 512), (1024, 512), (1536, 512), (2048, 192))
NT = (((1,), (1,)), ((), ()))
NN = (((1,), (0,)), ((), ()))


def _dot(a, b, dims):
    return lax.dot_general(a, b, dims, preferred_element_type=F32)


def _row(ref, n):
    vals = ref[...].astype(F32)
    return jnp.concatenate([vals[i:i + 1, :] for i in range(n)], axis=1)


def _rms(vals, gain):
    inv = lax.rsqrt(jnp.mean(vals * vals, axis=-1, keepdims=True) + EPS)
    return (vals * inv * gain).astype(BF16)


def attn_kernel(lens_s, x_ref, lens_ref, g_ref, bq_ref, bk_ref, bv_ref, freq_ref, wq_h, wk_h, wv_h, wo_h, k_h, v_h,
                part_ref, ko_h, vo_h,
                wq, wk, wv, wo, kbuf, vbuf, q_sc, kn_sc, vn_sc, len_sc, o_sc, wsem, ksem, vsem, kosem, vosem):
    def wcopy(i):
        src, dst = ((wq_h, wq), (wk_h, wk), (wv_h, wv), (wo_h, wo))[i]
        return pltpu.make_async_copy(src, dst, wsem.at[i])

    def rows(c):
        return pl.ds(pl.multiple_of(c * NB, NB), NB)

    def kin(c):
        return pltpu.make_async_copy(k_h.at[rows(c)], kbuf.at[rows(c)], ksem.at[c])

    def vin(c):
        return pltpu.make_async_copy(v_h.at[rows(c)], vbuf.at[rows(c)], vsem.at[c])

    def kout(c):
        return pltpu.make_async_copy(kbuf.at[rows(c)], ko_h.at[rows(c)], kosem.at[c])

    def vout(c):
        return pltpu.make_async_copy(vbuf.at[rows(c)], vo_h.at[rows(c)], vosem.at[c])

    for i in range(3):
        wcopy(i).start()
    for c in range(NCH):
        kin(c).start()
        vin(c).start()
    wcopy(3).start()

    normed = _rms(x_ref[...].astype(F32), _row(g_ref, D // 128))
    r_id = lax.broadcasted_iota(jnp.int32, (B, B), 0)
    c_id = lax.broadcasted_iota(jnp.int32, (B, B), 1)
    len_f = jnp.broadcast_to(lens_ref[...].astype(F32), (B, B))
    len_col = jnp.sum(jnp.where(r_id == c_id, len_f, 0.0), axis=1, keepdims=True)
    len_full = jnp.broadcast_to(len_col, (B, HD))
    len_sc[...] = len_full
    angles = len_full * freq_ref[...]
    cos = jnp.cos(angles)
    lane = lax.broadcasted_iota(jnp.int32, (B, HD), 1)
    sin = jnp.where(lane < HD // 2, -1.0, 1.0) * jnp.sin(angles)

    def rope(vals):
        out = vals * cos + pltpu.roll(vals, HD // 2, 1) * sin
        return out.astype(BF16).astype(F32)

    wcopy(0).wait()
    q_all = _dot(normed, wq[...], NN) + _row(bq_ref, G)
    for h in range(G):
        q_sc[h] = rope(q_all[:, h * HD:(h + 1) * HD])
    wcopy(1).wait()
    kn_sc[...] = rope(_dot(normed, wk[...], NN) + bk_ref[...].astype(F32))
    wcopy(2).wait()
    vn_sc[...] = (_dot(normed, wv[...], NN) + bv_ref[...].astype(F32)).astype(BF16).astype(F32)

    scale = HD ** -0.5
    sub16 = lax.broadcasted_iota(jnp.int32, (16, HD), 0)
    col_id = lax.broadcasted_iota(jnp.int32, (G * NB, L), 1).astype(F32)
    row_s = lax.broadcasted_iota(jnp.int32, (G * NB, L), 0) % NB
    row_o = lax.broadcasted_iota(jnp.int32, (G * NB, HD), 0) % NB

    def chunk(c, carry):
        r0 = pl.multiple_of(c * NB, NB)
        kin(c).wait()
        vin(c).wait()
        for b in range(NB):
            row = r0 + b
            length = lens_s[row]
            base = pl.multiple_of((length // 16) * 16, 16)
            hit = sub16 == length - base
            for buf, new in ((kbuf, kn_sc), (vbuf, vn_sc)):
                old = buf[row, pl.ds(base, 16), :].astype(F32)
                fresh = jnp.broadcast_to(new[pl.ds(row, 1), :], (16, HD))
                buf[row, pl.ds(base, 16), :] = jnp.where(hit, fresh, old).astype(BF16)
        q8 = jnp.concatenate([q_sc[h, pl.ds(r0, NB), :] for h in range(G)], axis=0).astype(BF16)
        scores = jnp.zeros((G * NB, L), F32)
        for b in range(NB):
            scores = jnp.where(row_s == b, _dot(q8, kbuf[r0 + b], NT), scores)
        len8 = len_sc[pl.ds(r0, NB), :]
        len24 = jnp.concatenate([len8] * G, axis=0)
        keep = col_id <= jnp.concatenate([len24] * (L // HD), axis=1)
        scores = jnp.where(keep, scores * scale, -jnp.inf)
        top = jnp.max(scores, axis=1, keepdims=True)
        exps = jnp.exp(scores - top)
        probs = (exps / jnp.sum(exps, axis=1, keepdims=True)).astype(BF16)
        out = jnp.zeros((G * NB, HD), F32)
        for b in range(NB):
            out = jnp.where(row_o == b, _dot(probs, vbuf[r0 + b], NN), out)
        for h in range(G):
            o_sc[pl.ds(r0, NB), h * HD:(h + 1) * HD] = out[h * NB:(h + 1) * NB, :]
        kout(c).start()
        vout(c).start()
        return carry

    lax.fori_loop(0, NCH, chunk, 0)
    wcopy(3).wait()
    part_ref[...] = _dot(o_sc[...].astype(BF16), wo[...], NN).astype(BF16)

    def drain(c, carry):
        kout(c).wait()
        vout(c).wait()
        return carry

    lax.fori_loop(0, NCH, drain, 0)


def attention(x, lens, k_cache, v_cache, g_attn, w_q, b_q, w_k, b_k, w_v, b_v, w_o):
    inv_freq = np.power(THETA, np.arange(HD // 2, dtype=np.float64) * (-2.0 / HD)).astype(np.float32)
    freq = jnp.asarray(np.concatenate([inv_freq, inv_freq])[None, :])
    vmem = pl.BlockSpec(memory_space=pltpu.VMEM)
    smem = pl.BlockSpec(memory_space=pltpu.SMEM)
    hbm = pl.BlockSpec(memory_space=pltpu.HBM)
    return pl.pallas_call(
        attn_kernel,
        name='attn',
        out_shape=(
            jax.ShapeDtypeStruct((B, D), BF16),
            jax.ShapeDtypeStruct((B, L, HD), BF16),
            jax.ShapeDtypeStruct((B, L, HD), BF16),
        ),
        in_specs=[smem] + [vmem] * 7 + [hbm] * 6,
        out_specs=(vmem, hbm, hbm),
        scratch_shapes=[
            pltpu.VMEM((D, G * HD), BF16),
            pltpu.VMEM((D, HD), BF16),
            pltpu.VMEM((D, HD), BF16),
            pltpu.VMEM((G * HD, D), BF16),
            pltpu.VMEM((B, L, HD), BF16),
            pltpu.VMEM((B, L, HD), BF16),
            pltpu.VMEM((G, B, HD), F32),
            pltpu.VMEM((B, HD), F32),
            pltpu.VMEM((B, HD), F32),
            pltpu.VMEM((B, HD), F32),
            pltpu.VMEM((B, G * HD), F32),
            pltpu.SemaphoreType.DMA((4,)),
            pltpu.SemaphoreType.DMA((NCH,)),
            pltpu.SemaphoreType.DMA((NCH,)),
            pltpu.SemaphoreType.DMA((NCH,)),
            pltpu.SemaphoreType.DMA((NCH,)),
        ],
        compiler_params=pltpu.CompilerParams(vmem_limit_bytes=40 * 1024 * 1024),
        cost_estimate=pl.CostEstimate(flops=400_000_000, bytes_accessed=37_000_000, transcendentals=0),
    )(lens, x, lens.reshape(1, B), g_attn.reshape(D // 128, 128), b_q.reshape(G, 128), b_k.reshape(1, 128),
      b_v.reshape(1, 128), freq, w_q, w_k, w_v, w_o, k_cache, v_cache)


def tail_kernel(part_ref, x_ref, gm_ref, gf_ref, tok_ref, wg_h, wu_h, wd_h, wh_h,
                y_ref, logp_ref, lse_ref,
                wg, wu, wd, wh, r1, ps, r2, abuf, h_sc, dpart, r3, ps2, r4, fall, toks, st_out, st_in,
                gsem, usem, dsem, hsem, send, recv, st_send, st_recv):
    dp = lax.axis_index('dp')
    tp = lax.axis_index('tp')
    core = tp % 2
    sib = tp + 1 - 2 * core
    xpeer = (tp + 2) % 4
    me = dp * NTP + tp
    ydp = dp + 1 - 2 * (dp % 2)
    zdp = (dp + 2) % 4
    ddp = (ydp + 2) % 4
    mine = pl.ds(pl.multiple_of(core * HALF, HALF), HALF)
    other = pl.ds(pl.multiple_of((1 - core) * HALF, HALF), HALF)

    def gcopy(i):
        s = pl.ds(*FF_CHUNKS[i])
        return pltpu.make_async_copy(wg_h.at[s], wg.at[s], gsem.at[i])

    def ucopy(i):
        s = pl.ds(*FF_CHUNKS[i])
        return pltpu.make_async_copy(wu_h.at[s], wu.at[s], usem.at[i])

    dcopy = pltpu.make_async_copy(wd_h, wd, dsem.at[0])
    v0 = dp * VQ - 8 * (dp // 3)

    def hcopy(j):
        src = wh_h.at[pl.ds(pl.multiple_of(v0 + j * VC, 8), VC)]
        return pltpu.make_async_copy(src, wh.at[pl.ds(pl.multiple_of(j * VC, VC), VC)], hsem.at[j])

    def remote(src, dst, i, **where):
        return pltpu.make_async_remote_copy(src_ref=src, dst_ref=dst, send_sem=send.at[i], recv_sem=recv.at[i],
                                            device_id=where, device_id_type=MESH)

    for i in range(len(FF_CHUNKS)):
        gcopy(i).start()
        ucopy(i).start()
    dcopy.start()

    tok2 = jnp.concatenate([tok_ref[...], tok_ref[...]], axis=1)
    toks[dp] = jnp.broadcast_to(tok2, (8, 128))

    barrier = pltpu.get_barrier_semaphore()
    for k in range(1, NDP * NTP):
        there = (me + k) % (NDP * NTP)
        pl.semaphore_signal(barrier, inc=1, device_id={'dp': there // NTP, 'tp': there % NTP}, device_id_type=MESH)
    pl.semaphore_wait(barrier, NDP * NTP - 1)

    c0 = remote(part_ref.at[other], r1, 0, tp=sib)
    c0.start()
    tok_copies = [remote(toks.at[dp], toks.at[dp], 13 + i, dp=d) for i, d in enumerate((ydp, zdp, ddp))]
    for c in tok_copies:
        c.start()
    c0.wait()
    ps[...] = (part_ref[mine, :].astype(F32) + r1[...].astype(F32)).astype(BF16)
    c1 = remote(ps, r2, 1, tp=xpeer)
    c1.start()
    gain_m = _row(gm_ref, D // 128)
    gain_f = _row(gf_ref, D // 128)
    c1.wait()
    a_half = (x_ref[mine, :].astype(F32) + (ps[...].astype(F32) + r2[...].astype(F32))).astype(BF16)
    abuf[mine, :] = a_half
    c2 = remote(abuf.at[mine], abuf.at[mine], 2, tp=sib)
    c2.start()
    c2.wait()

    mlp_in = _rms(abuf[...].astype(F32), gain_m)
    for i, (s, n) in enumerate(FF_CHUNKS):
        gcopy(i).wait()
        gate = _dot(mlp_in, wg[s:s + n, :], NT)
        ucopy(i).wait()
        up = _dot(mlp_in, wu[s:s + n, :], NT)
        h_sc[:, s:s + n] = (gate * (1.0 / (1.0 + jnp.exp(-gate))) * up).astype(BF16)
    dcopy.wait()
    for j in range(NVC):
        hcopy(j).start()
    dpart[...] = _dot(h_sc[...], wd[...], NN).astype(BF16)

    c3 = remote(dpart.at[other], r3, 3, tp=sib)
    c3.start()
    c3.wait()
    ps2[...] = (dpart[mine, :].astype(F32) + r3[...].astype(F32)).astype(BF16)
    c4 = remote(ps2, r4, 4, tp=xpeer)
    c4.start()
    c4.wait()
    y_half = (abuf[mine, :].astype(F32) + (ps2[...].astype(F32) + r4[...].astype(F32))).astype(BF16)
    y_ref[mine, :] = y_half

    def frows(d, c):
        return pl.ds(pl.multiple_of(d * B + c * HALF, HALF), HALF)

    own = frows(dp, core)
    fall[own, :] = _rms(y_half.astype(F32), gain_f)
    gathers = [remote(fall.at[own], fall.at[own], 7 + i, dp=d) for i, d in enumerate((ydp, zdp, ddp))]
    for c in gathers:
        c.start()
    c6 = remote(fall.at[own], fall.at[own], 6, tp=sib)
    c6.start()
    c5 = remote(y_ref.at[mine], y_ref.at[mine], 5, tp=sib)
    c5.start()
    forwards = []
    for i, d in enumerate((ydp, zdp, ddp)):
        gathers[i].wait_recv()
        fwd = remote(fall.at[frows(d, core)], fall.at[frows(d, core)], 10 + i, tp=sib)
        fwd.start()
        forwards.append(fwd)
    for c in tok_copies:
        c.wait()
    lane = lax.broadcasted_iota(jnp.int32, (8, 128), 1)
    lo = jnp.where(lane < B, toks[0], toks[1])
    hi = jnp.where(lane < B, toks[2], toks[3])
    want = jnp.concatenate([lo, hi], axis=1) - (tp * VOC + v0)
    first = 8 * (dp // 3)
    want = jnp.where((want >= first) & (want < first + VQ), want, -1)
    for c in gathers:
        c.wait_send()
    for c in forwards + [c5, c6]:
        c.wait()

    sub = lax.broadcasted_iota(jnp.int32, (VC // 8, 8, NDP * B), 0) * 8 + lax.broadcasted_iota(
        jnp.int32, (VC // 8, 8, NDP * B), 1)

    def vocab(j, carry):
        top, total, target = carry
        hcopy(j).wait()
        z = _dot(wh[pl.ds(pl.multiple_of(j * VC, VC), VC), :], fall[...], NT)
        drop_first = (first > 0) & (j == 0)
        drop_last = (first == 0) & (j == NVC - 1)
        z = jnp.concatenate([
            jnp.where(drop_first, -jnp.inf, z[:8]), z[8:VC - 8], jnp.where(drop_last, -jnp.inf, z[VC - 8:])], axis=0)
        z = z.reshape(VC // 8, 8, NDP * B)
        new_top = jnp.maximum(top, jnp.max(z, axis=0))
        total = total * jnp.exp(top - new_top) + jnp.sum(jnp.exp(z - new_top[None]), axis=0)
        hit = sub == (want - j * VC)[None]
        target = target + jnp.sum(jnp.where(hit, z, 0.0), axis=0)
        return new_top, total, target

    top, total, target = lax.fori_loop(0, NVC, vocab, (
        jnp.full((8, NDP * B), -jnp.inf, F32), jnp.zeros((8, NDP * B), F32), jnp.zeros((8, NDP * B), F32)))

    t_row = jnp.max(top, axis=0, keepdims=True)
    s_row = jnp.sum(total * jnp.exp(top - t_row), axis=0, keepdims=True)
    z_row = jnp.sum(target, axis=0, keepdims=True)
    row8 = lax.broadcasted_iota(jnp.int32, (8, NDP * B), 0)
    stats = jnp.where(row8 == 0, t_row, jnp.where(row8 == 1, s_row, z_row))
    st_out[0] = stats[:, :128]
    st_out[1] = stats[:, 128:]
    st_in[me] = jnp.where(dp // 2 == 0, stats[:, :128], stats[:, 128:])
    st_copies = []
    for k in range(1, NDP * NTP):
        there = (me + k) % (NDP * NTP)
        c = pltpu.make_async_remote_copy(
            src_ref=st_out.at[there // NTP // 2], dst_ref=st_in.at[me], send_sem=st_send.at[k],
            recv_sem=st_recv.at[k], device_id={'dp': there // NTP, 'tp': there % NTP}, device_id_type=MESH)
        c.start()
        st_copies.append(c)
    for c in st_copies:
        c.wait()
    every = st_in[...]
    tops = every[:, 0:1, :]
    best = jnp.max(tops, axis=0)
    mass = jnp.sum(every[:, 1:2, :] * jnp.exp(tops - best[None]), axis=0)
    hits = jnp.sum(every[:, 2:3, :], axis=0)
    lse = best + jnp.log(mass)
    logp = hits - lse
    left = dp % 2 == 0
    lse_ref[...] = jnp.where(left, lse[:, :B], lse[:, B:])
    logp_ref[...] = jnp.where(left, logp[:, :B], logp[:, B:])


def tail(part, x, g_mlp, g_final, next_tok, w_gate, w_up, w_down, w_head):
    vmem = pl.BlockSpec(memory_space=pltpu.VMEM)
    hbm = pl.BlockSpec(memory_space=pltpu.HBM)
    nff = len(FF_CHUNKS)
    half = pltpu.VMEM((HALF, D), BF16)
    return pl.pallas_call(
        tail_kernel,
        name='tail',
        out_shape=(
            jax.ShapeDtypeStruct((B, D), BF16),
            jax.ShapeDtypeStruct((1, B), F32),
            jax.ShapeDtypeStruct((1, B), F32),
        ),
        in_specs=[vmem] * 5 + [hbm] * 4,
        out_specs=(vmem, vmem, vmem),
        scratch_shapes=[
            pltpu.VMEM((FF, D), BF16),
            pltpu.VMEM((FF, D), BF16),
            pltpu.VMEM((FF, D), BF16),
            pltpu.VMEM((VC * NVC, D), BF16),
            half, half, half,
            pltpu.VMEM((B, D), BF16),
            pltpu.VMEM((B, FF), BF16),
            pltpu.VMEM((B, D), BF16),
            half, half, half,
            pltpu.VMEM((NDP * B, D), BF16),
            pltpu.VMEM((NDP, 8, 128), jnp.int32),
            pltpu.VMEM((2, 8, 128), F32),
            pltpu.VMEM((NDP * NTP, 8, 128), F32),
            pltpu.SemaphoreType.DMA((nff,)),
            pltpu.SemaphoreType.DMA((nff,)),
            pltpu.SemaphoreType.DMA((1,)),
            pltpu.SemaphoreType.DMA((NVC,)),
            pltpu.SemaphoreType.DMA((16,)),
            pltpu.SemaphoreType.DMA((16,)),
            pltpu.SemaphoreType.DMA((16,)),
            pltpu.SemaphoreType.DMA((16,)),
        ],
        compiler_params=pltpu.CompilerParams(
            vmem_limit_bytes=61 * 1024 * 1024, collective_id=0, has_side_effects=True),
        cost_estimate=pl.CostEstimate(flops=10_000_000_000, bytes_accessed=50_000_000, transcendentals=0),
    )(part, x, g_mlp.reshape(D // 128, 128), g_final.reshape(D // 128, 128), next_tok.reshape(1, B),
      w_gate.T, w_up.T, w_down, w_head)


def local_step(tok_hidden, seq_lens, k_cache, v_cache, next_tok, g_attn, w_q, b_q, w_k, b_k, w_v, b_v, w_o, g_mlp,
               w_gate, w_up, w_down, g_final, w_head):
    part, k_all, v_all = attention(
        tok_hidden, seq_lens, k_cache.reshape(B, L, HD), v_cache.reshape(B, L, HD), g_attn, w_q, b_q, w_k, b_k, w_v,
        b_v, w_o)
    y_out, tok_logp, norm_lse = tail(part, tok_hidden, g_mlp, g_final, next_tok, w_gate, w_up, w_down, w_head)
    return (y_out, k_all.reshape(B, L, 1, HD), v_all.reshape(B, L, 1, HD), tok_logp.reshape(B), norm_lse.reshape(B))


def solution(mesh):
    row_spec = P('dp', None)
    vec_spec = P('dp')
    cache_spec = P('dp', None, 'tp', None)
    col_spec = P(None, 'tp')
    part_spec = P('tp')
    whole_spec = P(None)
    in_specs = (row_spec, vec_spec, cache_spec, cache_spec, vec_spec, whole_spec, col_spec, part_spec, col_spec,
                part_spec, col_spec, part_spec, P('tp', None), whole_spec, col_spec, col_spec, P('tp', None),
                whole_spec, P('tp', None))
    out_specs = (row_spec, cache_spec, cache_spec, vec_spec, vec_spec)
    return jax.shard_map(local_step, mesh=mesh, in_specs=in_specs, out_specs=out_specs, check_vma=False)
```

time: 185 us -> 80.6 us (0.44)
  matrix products: 78.4 us -> 0 us
  Pallas kernels: 0 us -> 62.1 us
  waiting for transfers between devices: 59.3 us -> 0 us
  other arithmetic: 26.8 us -> 0 us
  local copies, waits for them, and re-layouts: 0.09 us -> 17.4 us
  between operations: 14.3 us -> 0.68 us
  blocking collectives: 5.17 us -> 0 us
    dot_general x8 -> x0, matrix products: 72.5 us -> none  [the longest x1 48 us: local_step(): lax.dot_general(final_norm, w_head, (((1,), (1,)), ((), ())), preferred_e...]
    pallas_call x0 -> x2, Pallas kernels: none -> 62.1 us  [the longest x1 50.1 us: tail(): pl.pallas_call(tail_kernel, name='tail', out_shape=(jax.ShapeDtypeStruct(...]
    psum x2 -> x0, waiting for transfers between devices: 59.2 us -> none  [the longest x1 30.9 us: local_step(): attn_sum = lax.psum(attn_part, 'tp')]
    unnamed x14 -> x29, local copies, waits for them, and re-layouts: 0.05 us -> 17.4 us
    select_n x1 -> x0, other arithmetic: 11.9 us -> none  [attention_block(): k_all = jnp.where(write_mask, k_new[:, None], k_cache)]
    reduce_sum x5 -> x0, other arithmetic: 9.46 us -> none  [the longest x1 6.17 us: local_step(): local_sum = jnp.sum(jnp.exp(logits - local_max[:, None]), axis=1)]
    sub x1 -> x0, matrix products: 5.9 us -> none  [attention_block(): exp_scores = jnp.exp(scores - row_max)]
    all_gather x1 -> x0, blocking collectives: 5.17 us -> none  [local_step(): lax.all_gather(jnp.stack([local_max, local_sum, local_target]), 'tp')]
  transfers between devices with their start and end apart: 2 -> 0, of which waited for: 2 -> 0; matrix products, arithmetic and copies ran while one was open for 0% -> 0% of each run, Pallas kernels for 0% -> 0%
where the time goes in v1:
time: 80.6 us; the launch traced here: 80.1 us
  Pallas kernels  62.1 us (77%)
  local copies, waits for them, and re-layouts  17.4 us (22%)
    pallas_call x1, Pallas kernels, tail(): pl.pallas_call(tail_kernel, name='tail', out_shape=(jax.ShapeDtypeStruct(...  50.1 us
    unnamed x29, local copies, waits for them, and re-layouts  17.4 us
    pallas_call x1, Pallas kernels, attention(): pl.pallas_call(attn_kernel, name='attn', out_shape=(jax.ShapeDtypeStruct(...  11.9 us

profile of v1, /device:TPU:0, one launch (start us, length us, event | category | flops | bytes accessed | tf_op | source)
XLA Modules:
  0.0 80.1 jit_solution(10857936043297928541)
XLA Ops:
  0.6 0.0 copy-start
  0.6 3.4 %copy-done = bf16[64,512,1,128]{3,1,2,0:T(8,128)(2,1)S(1)} copy-done((bf16[64,512,1,128]{3,1,2,0:T(8,128)(2,1)S(1)}, bf16[64,512,1,128]{3,1,2,0:T(8,128)(2,1)}, u32[]{:S(2)}) %copy-start) | copy-done | bytes 8388632
  4.0 0.0 copy-start.1
  4.0 1.3 %copy-done.1 = bf16[1536,384]{1,0:T(8,128)(2,1)S(1)} copy-done((bf16[1536,384]{1,0:T(8,128)(2,1)S(1)}, bf16[1536,384]{1,0:T(8,128)(2,1)}, u32[]{:S(2)}) %copy-start.1) | copy-done | bytes 1179672
  5.3 0.0 copy-start.2
  5.3 1.3 %copy-done.2 = bf16[384,1536]{1,0:T(8,128)(2,1)S(1)} copy-done((bf16[384,1536]{1,0:T(8,128)(2,1)S(1)}, bf16[384,1536]{1,0:T(8,128)(2,1)}, u32[]{:S(2)}) %copy-start.2) | copy-done | bytes 1179672
  6.6 0.0 copy-start.3
  6.6 0.9 %copy-done.3 = bf16[64,1536]{1,0:T(8,128)(2,1)S(1)} copy-done((bf16[64,1536]{1,0:T(8,128)(2,1)S(1)}, bf16[64,1536]{1,0:T(8,128)(2,1)}, u32[]{:S(2)}) %copy-start.3) | copy-done | bytes 196632
  7.5 0.0 copy-start.4
  7.5 1.0 %copy-done.4 = bf16[1536,128]{1,0:T(8,128)(2,1)S(1)} copy-done((bf16[1536,128]{1,0:T(8,128)(2,1)S(1)}, bf16[1536,128]{1,0:T(8,128)(2,1)}, u32[]{:S(2)}) %copy-start.4) | copy-done | bytes 393240
  8.5 0.0 copy-start.5
  8.5 1.0 %copy-done.5 = bf16[1536,128]{1,0:T(8,128)(2,1)S(1)} copy-done((bf16[1536,128]{1,0:T(8,128)(2,1)S(1)}, bf16[1536,128]{1,0:T(8,128)(2,1)}, u32[]{:S(2)}) %copy-start.5) | copy-done | bytes 393240
  9.5 0.0 copy-start.7
  9.5 0.7 copy-done.7
  10.2 0.0 copy-start.8
  10.2 0.7 copy-done.8
  10.8 0.0 copy-start.9
  10.8 0.7 copy-done.9
  11.5 0.0 copy-start.10
  11.5 0.7 copy-done.10
  12.2 0.0 copy-start.11
  12.2 0.7 copy-done.11
  12.8 0.0 copy-start.12
  12.8 0.7 copy-done.12
  13.5 11.9 %attn.1 = (bf16[64,1536]{1,0:T(8,128)(2,1)S(1)}, bf16[64,512,128]{2,1,0:T(8,128)(2,1)}, bf16[64,512,128]{2,1,0:T(8,128)(2,1)}) custom-call(s32[64]{0:T(128)S(1)} %copy-done.8, bf16[64,1536]{1,0:T(8,128)(2,1)S(1)} %copy-done.3, s32[1,64]{1,0:T(1,128)S(1)} %bitcast.22, bf16[12,128]{1,0:T(8,128)(2,1)S(1)} %bitcast.21, bf16[3,128]{1,0:T(4,128)(2,1)S(1)} %bitcast.23, ...), custom_call_target="tpu_custom_call" | custom-call | flops 400000000 | bytes 37000000 | tf_op jit(solution)/shard_map/attn/pallas_call | solution.py:162
  25.4 0.0 copy-start.6
  25.4 0.7 copy-done.6
  26.1 50.1 %tail.1 = (bf16[64,1536]{1,0:T(8,128)(2,1)}, f32[1,64]{1,0:T(1,128)}, f32[1,64]{1,0:T(1,128)}) custom-call(bf16[64,1536]{1,0:T(8,128)(2,1)} %copy-done.6, bf16[64,1536]{1,0:T(8,128)(2,1)} %x_ref.3, bf16[12,128]{1,0:T(8,128)(2,1)} %bitcast.29, bf16[12,128]{1,0:T(8,128)(2,1)} %bitcast.30, s32[1,64]{1,0:T(1,128)} %bitcast.31, bf16[2240,1536]{1,0:T(8,128)(2,1)} %bitcast.27, ...), custom_call_target="tpu_custom_call" | custom-call | flops 10000000000 | bytes 50000000 | tf_op jit(solution)/shard_map/tail/pallas_call | solution.py:372
  76.2 1.6 %copy.30 = bf16[64,1536]{1,0:T(8,128)(2,1)} copy(bf16[64,1536]{1,0:T(8,128)(2,1)} %get-tuple-element.27) | data formatting | bytes 393216
  77.9 1.1 %copy.31 = f32[64]{0:T(128)} copy(f32[64]{0:T(128)} %bitcast.35) | data formatting | bytes 512
  79.0 1.2 %copy.32 = f32[64]{0:T(128)} copy(f32[64]{0:T(128)} %bitcast.34) | data formatting | bytes 512
Async XLA Ops:
  0.6 3.4 %copy-start = (bf16[64,512,1,128]{3,1,2,0:T(8,128)(2,1)S(1)}, bf16[64,512,1,128]{3,1,2,0:T(8,128)(2,1)}, u32[]{:S(2)}) copy-start(bf16[64,512,1,128]{3,1,2,0:T(8,128)(2,1)} %param.22) | copy-start | bytes 25165828
  4.0 1.3 %copy-start.1 = (bf16[1536,384]{1,0:T(8,128)(2,1)S(1)}, bf16[1536,384]{1,0:T(8,128)(2,1)}, u32[]{:S(2)}) copy-start(bf16[1536,384]{1,0:T(8,128)(2,1)} %wq_h.1) | copy-start | bytes 3538948
  5.3 1.3 %copy-start.2 = (bf16[384,1536]{1,0:T(8,128)(2,1)S(1)}, bf16[384,1536]{1,0:T(8,128)(2,1)}, u32[]{:S(2)}) copy-start(bf16[384,1536]{1,0:T(8,128)(2,1)} %wo_h.1) | copy-start | bytes 3538948
  6.6 0.9 %copy-start.3 = (bf16[64,1536]{1,0:T(8,128)(2,1)S(1)}, bf16[64,1536]{1,0:T(8,128)(2,1)}, u32[]{:S(2)}) copy-start(bf16[64,1536]{1,0:T(8,128)(2,1)} %x_ref.3) | copy-start | bytes 589828
  7.5 1.0 %copy-start.4 = (bf16[1536,128]{1,0:T(8,128)(2,1)S(1)}, bf16[1536,128]{1,0:T(8,128)(2,1)}, u32[]{:S(2)}) copy-start(bf16[1536,128]{1,0:T(8,128)(2,1)} %wk_h.1) | copy-start | bytes 1179652
  8.5 1.0 %copy-start.5 = (bf16[1536,128]{1,0:T(8,128)(2,1)S(1)}, bf16[1536,128]{1,0:T(8,128)(2,1)}, u32[]{:S(2)}) copy-start(bf16[1536,128]{1,0:T(8,128)(2,1)} %wv_h.1) | copy-start | bytes 1179652
  9.5 0.7 copy-start.7
  10.2 0.7 copy-start.8
  10.8 0.7 copy-start.9
  11.5 0.7 copy-start.10
  12.2 0.7 copy-start.11
  12.8 0.7 copy-start.12
  25.4 0.7 copy-start.6

commit v2 on v1

v2 whole, which is shorter than its diff:
```python
import functools
import math
import jax
import jax.numpy as jnp
import numpy as np
from jax import lax
from jax.experimental import pallas as pl
from jax.experimental.pallas import tpu as pltpu
from jax.sharding import PartitionSpec as P

THETA = 1000000.0
EPS = 1e-6
MESH = pl.DeviceIdType.MESH
F32 = jnp.float32
BF16 = jnp.bfloat16

B = 64
L = 512
D = 1536
HD = 128
G = 3
FF = 2240
VOC = 37984
NDP = 4
NTP = 4
NB = 8
NCH = B // NB
AHEAD = 3
VQ = VOC // NDP
VC = 528
NVC = 18
UNROLL = 6
HALF = B // 2
FF_CHUNKS = ((0, 512), (512, 512), (1024, 512), (1536, 512), (2048, 192))
NT = (((1,), (1,)), ((), ()))
NN = (((1,), (0,)), ((), ()))


def _dot(a, b, dims):
    return lax.dot_general(a, b, dims, preferred_element_type=F32)


def _row(ref, n):
    vals = ref[...].astype(F32)
    return jnp.concatenate([vals[i:i + 1, :] for i in range(n)], axis=1)


def _rms(vals, gain):
    inv = lax.rsqrt(jnp.mean(vals * vals, axis=-1, keepdims=True) + EPS)
    return (vals * inv * gain).astype(BF16)


def attn_kernel(x_h, lens_h, g_h, bq_h, bk_h, bv_h, freq_h, wq_h, wk_h, wv_h, wo_h, k_h, v_h,
                part_ref, ko_h, vo_h,
                lens_s, x_ref, lens_ref, g_ref, bq_ref, bk_ref, bv_ref, freq_ref,
                wq, wk, wv, wo, kbuf, vbuf, q_sc, kn_sc, vn_sc, len_sc, o_sc, isem, wsem, ksem, vsem, kosem, vosem):
    small = [pltpu.make_async_copy(src, dst, isem.at[i]) for i, (src, dst) in enumerate((
        (x_h, x_ref), (g_h, g_ref), (lens_h, lens_ref), (freq_h, freq_ref), (bq_h, bq_ref), (bk_h, bk_ref),
        (bv_h, bv_ref), (lens_h, lens_s)))]

    def wcopy(i):
        src, dst = ((wq_h, wq), (wk_h, wk), (wv_h, wv), (wo_h, wo))[i]
        return pltpu.make_async_copy(src, dst, wsem.at[i])

    def rows(c):
        return pl.ds(pl.multiple_of(c * NB, NB), NB)

    def kin(c):
        return pltpu.make_async_copy(k_h.at[rows(c)], kbuf.at[rows(c)], ksem.at[c])

    def vin(c):
        return pltpu.make_async_copy(v_h.at[rows(c)], vbuf.at[rows(c)], vsem.at[c])

    def kout(c):
        return pltpu.make_async_copy(kbuf.at[rows(c)], ko_h.at[rows(c)], kosem.at[c])

    def vout(c):
        return pltpu.make_async_copy(vbuf.at[rows(c)], vo_h.at[rows(c)], vosem.at[c])

    with jax.named_scope('starts'):
        for c in small:
            c.start()
        for i in range(3):
            wcopy(i).start()
        for c in range(AHEAD):
            kin(c).start()
            vin(c).start()

    with jax.named_scope('qkv'):
        for c in small:
            c.wait()
        normed = _rms(x_ref[...].astype(F32), _row(g_ref, D // 128))
        r_id = lax.broadcasted_iota(jnp.int32, (B, B), 0)
        c_id = lax.broadcasted_iota(jnp.int32, (B, B), 1)
        len_f = jnp.broadcast_to(lens_ref[...].astype(F32), (B, B))
        len_col = jnp.sum(jnp.where(r_id == c_id, len_f, 0.0), axis=1, keepdims=True)
        len_full = jnp.broadcast_to(len_col, (B, HD))
        len_sc[...] = len_full
        angles = len_full * freq_ref[...]
        cos = jnp.cos(angles)
        lane = lax.broadcasted_iota(jnp.int32, (B, HD), 1)
        sin = jnp.where(lane < HD // 2, -1.0, 1.0) * jnp.sin(angles)

        def rope(vals):
            out = vals * cos + pltpu.roll(vals, HD // 2, 1) * sin
            return out.astype(BF16).astype(F32)

        wcopy(0).wait()
        q_all = _dot(normed, wq[...], NN) + _row(bq_ref, G)
        for h in range(G):
            q_sc[h] = rope(q_all[:, h * HD:(h + 1) * HD])
        wcopy(1).wait()
        kn_sc[...] = rope(_dot(normed, wk[...], NN) + bk_ref[...].astype(F32))
        wcopy(2).wait()
        vn_sc[...] = (_dot(normed, wv[...], NN) + bv_ref[...].astype(F32)).astype(BF16).astype(F32)

    scale = HD ** -0.5
    sub16 = lax.broadcasted_iota(jnp.int32, (16, HD), 0)
    col_id = lax.broadcasted_iota(jnp.int32, (G * NB, L), 1).astype(F32)
    row_s = lax.broadcasted_iota(jnp.int32, (G * NB, L), 0) % NB
    row_o = lax.broadcasted_iota(jnp.int32, (G * NB, HD), 0) % NB

    def chunk(c, carry):
        r0 = pl.multiple_of(c * NB, NB)
        kin(c).wait()
        vin(c).wait()

        @pl.when(c + AHEAD < NCH)
        def _():
            kin(c + AHEAD).start()
            vin(c + AHEAD).start()

        @pl.when(c + AHEAD == NCH)
        def _():
            wcopy(3).start()

        for b in range(NB):
            row = r0 + b
            length = lens_s[0, row]
            base = pl.multiple_of((length // 16) * 16, 16)
            hit = sub16 == length - base
            for buf, new in ((kbuf, kn_sc), (vbuf, vn_sc)):
                old = buf[row, pl.ds(base, 16), :].astype(F32)
                fresh = jnp.broadcast_to(new[pl.ds(row, 1), :], (16, HD))
                buf[row, pl.ds(base, 16), :] = jnp.where(hit, fresh, old).astype(BF16)
        q8 = jnp.concatenate([q_sc[h, pl.ds(r0, NB), :] for h in range(G)], axis=0).astype(BF16)
        scores = jnp.zeros((G * NB, L), F32)
        for b in range(NB):
            scores = jnp.where(row_s == b, _dot(q8, kbuf[r0 + b], NT), scores)
        len8 = len_sc[pl.ds(r0, NB), :]
        len24 = jnp.concatenate([len8] * G, axis=0)
        keep = col_id <= jnp.concatenate([len24] * (L // HD), axis=1)
        scores = jnp.where(keep, scores * scale, -jnp.inf)
        top = jnp.max(scores, axis=1, keepdims=True)
        exps = jnp.exp(scores - top)
        probs = (exps / jnp.sum(exps, axis=1, keepdims=True)).astype(BF16)
        out = jnp.zeros((G * NB, HD), F32)
        for b in range(NB):
            out = jnp.where(row_o == b, _dot(probs, vbuf[r0 + b], NN), out)
        for h in range(G):
            o_sc[pl.ds(r0, NB), h * HD:(h + 1) * HD] = out[h * NB:(h + 1) * NB, :]
        kout(c).start()
        vout(c).start()
        return carry

    with jax.named_scope('cache'):
        lax.fori_loop(0, NCH, chunk, 0)
    with jax.named_scope('proj'):
        wcopy(3).wait()
        part_ref[...] = _dot(o_sc[...].astype(BF16), wo[...], NN).astype(BF16)

    def drain(c, carry):
        kout(c).wait()
        vout(c).wait()
        return carry

    with jax.named_scope('drain'):
        lax.fori_loop(0, NCH, drain, 0)


def attention(x, lens, k_cache, v_cache, g_attn, w_q, b_q, w_k, b_k, w_v, b_v, w_o):
    inv_freq = np.power(THETA, np.arange(HD // 2, dtype=np.float64) * (-2.0 / HD)).astype(np.float32)
    freq = jnp.asarray(np.concatenate([inv_freq, inv_freq])[None, :])
    vmem = pl.BlockSpec(memory_space=pltpu.VMEM)
    hbm = pl.BlockSpec(memory_space=pltpu.HBM)
    return pl.pallas_call(
        attn_kernel,
        name='attn',
        out_shape=(
            jax.ShapeDtypeStruct((B, D), BF16),
            jax.ShapeDtypeStruct((B, L, HD), BF16),
            jax.ShapeDtypeStruct((B, L, HD), BF16),
        ),
        in_specs=[hbm] * 13,
        out_specs=(vmem, hbm, hbm),
        scratch_shapes=[
            pltpu.SMEM((1, B), jnp.int32),
            pltpu.VMEM((B, D), BF16),
            pltpu.VMEM((1, B), jnp.int32),
            pltpu.VMEM((D // 128, 128), BF16),
            pltpu.VMEM((G, 128), BF16),
            pltpu.VMEM((1, 128), BF16),
            pltpu.VMEM((1, 128), BF16),
            pltpu.VMEM((1, 128), F32),
            pltpu.VMEM((D, G * HD), BF16),
            pltpu.VMEM((D, HD), BF16),
            pltpu.VMEM((D, HD), BF16),
            pltpu.VMEM((G * HD, D), BF16),
            pltpu.VMEM((B, L, HD), BF16),
            pltpu.VMEM((B, L, HD), BF16),
            pltpu.VMEM((G, B, HD), F32),
            pltpu.VMEM((B, HD), F32),
            pltpu.VMEM((B, HD), F32),
            pltpu.VMEM((B, HD), F32),
            pltpu.VMEM((B, G * HD), F32),
            pltpu.SemaphoreType.DMA((8,)),
            pltpu.SemaphoreType.DMA((4,)),
            pltpu.SemaphoreType.DMA((NCH,)),
            pltpu.SemaphoreType.DMA((NCH,)),
            pltpu.SemaphoreType.DMA((NCH,)),
            pltpu.SemaphoreType.DMA((NCH,)),
        ],
        compiler_params=pltpu.CompilerParams(vmem_limit_bytes=62 * 1024 * 1024),
        cost_estimate=pl.CostEstimate(flops=400_000_000, bytes_accessed=37_000_000, transcendentals=0),
    )(x, lens.reshape(1, B), g_attn.reshape(D // 128, 128), b_q.reshape(G, 128), b_k.reshape(1, 128),
      b_v.reshape(1, 128), freq, w_q, w_k, w_v, w_o, k_cache, v_cache)


def tail_kernel(part_h, x_h, gm_h, gf_h, tok_h, wg_h, wu_h, wd_h, wh_h,
                y_h, st_in,
                part_ref, x_ref, gm_ref, gf_ref, tok_ref, y_ref, wg, wu, wd, wh, r1, ps, r2, abuf, h_sc, dpart, r3, ps2, r4, fall, toks, st_out,
                isem, gsem, usem, dsem, hsem, send, recv, st_send, st_recv):
    dp = lax.axis_index('dp')
    tp = lax.axis_index('tp')
    core = tp % 2
    sib = tp + 1 - 2 * core
    xpeer = (tp + 2) % 4
    me = dp * NTP + tp
    ydp = dp + 1 - 2 * (dp % 2)
    zdp = (dp + 2) % 4
    ddp = (ydp + 2) % 4
    mine = pl.ds(pl.multiple_of(core * HALF, HALF), HALF)
    other = pl.ds(pl.multiple_of((1 - core) * HALF, HALF), HALF)

    def gcopy(i):
        s = pl.ds(*FF_CHUNKS[i])
        return pltpu.make_async_copy(wg_h.at[s], wg.at[s], gsem.at[i])

    def ucopy(i):
        s = pl.ds(*FF_CHUNKS[i])
        return pltpu.make_async_copy(wu_h.at[s], wu.at[s], usem.at[i])

    dcopy = pltpu.make_async_copy(wd_h, wd, dsem.at[0])
    v0 = dp * VQ - 8 * (dp // 3)

    def hcopy(j):
        src = wh_h.at[pl.ds(pl.multiple_of(v0 + j * VC, 8), VC)]
        return pltpu.make_async_copy(src, wh.at[pl.ds(pl.multiple_of(j * VC, VC), VC)], hsem.at[j])

    def remote(src, dst, i, **where):
        return pltpu.make_async_remote_copy(src_ref=src, dst_ref=dst, send_sem=send.at[i], recv_sem=recv.at[i],
                                            device_id=where, device_id_type=MESH)

    small = [pltpu.make_async_copy(src, dst, isem.at[i]) for i, (src, dst) in enumerate((
        (part_h, part_ref), (tok_h, tok_ref), (x_h, x_ref), (gm_h, gm_ref), (gf_h, gf_ref)))]
    y_out = pltpu.make_async_copy(y_ref, y_h, isem.at[5])
    barrier = pltpu.get_barrier_semaphore()
    for k in range(1, NDP * NTP):
        there = (me + k) % (NDP * NTP)
        pl.semaphore_signal(barrier, inc=1, device_id={'dp': there // NTP, 'tp': there % NTP}, device_id_type=MESH)
    for c in small:
        c.start()
    gcopy(0).start()
    for c in small:
        c.wait()
    ucopy(0).start()
    for i in range(1, len(FF_CHUNKS)):
        gcopy(i).start()
        ucopy(i).start()
    dcopy.start()

    tok2 = jnp.concatenate([tok_ref[...], tok_ref[...]], axis=1)
    toks[dp] = jnp.broadcast_to(tok2, (8, 128))

    with jax.named_scope('barrier'):
        pl.semaphore_wait(barrier, NDP * NTP - 1)

    with jax.named_scope('sum1'):
        c0 = remote(part_ref.at[other], r1, 0, tp=sib)
        c0.start()
        tok_copies = [remote(toks.at[dp], toks.at[dp], 13 + i, dp=d) for i, d in enumerate((ydp, zdp, ddp))]
        for c in tok_copies:
            c.start()
        c0.wait()
        ps[...] = (part_ref[mine, :].astype(F32) + r1[...].astype(F32)).astype(BF16)
        c1 = remote(ps, r2, 1, tp=xpeer)
        c1.start()
        gain_m = _row(gm_ref, D // 128)
        gain_f = _row(gf_ref, D // 128)
        c1.wait()
        a_half = (x_ref[mine, :].astype(F32) + (ps[...].astype(F32) + r2[...].astype(F32))).astype(BF16)
        abuf[mine, :] = a_half
        c2 = remote(abuf.at[mine], abuf.at[mine], 2, tp=sib)
        c2.start()
        c2.wait()

    with jax.named_scope('mlp'):
        mlp_in = _rms(abuf[...].astype(F32), gain_m)
        for i in range(len(FF_CHUNKS)):
            gcopy(i).wait()
            ucopy(i).wait()
        dcopy.wait()
        for j in range(NVC):
            hcopy(j).start()
        for s, n in FF_CHUNKS:
            gate = _dot(mlp_in, wg[s:s + n, :], NT)
            up = _dot(mlp_in, wu[s:s + n, :], NT)
            h_sc[:, s:s + n] = (gate * (1.0 / (1.0 + jnp.exp(-gate))) * up).astype(BF16)
        dpart[...] = _dot(h_sc[...], wd[...], NN).astype(BF16)

    with jax.named_scope('sum2'):
        c3 = remote(dpart.at[other], r3, 3, tp=sib)
        c3.start()
        c3.wait()
        ps2[...] = (dpart[mine, :].astype(F32) + r3[...].astype(F32)).astype(BF16)
        c4 = remote(ps2, r4, 4, tp=xpeer)
        c4.start()
        c4.wait()
        y_half = (abuf[mine, :].astype(F32) + (ps2[...].astype(F32) + r4[...].astype(F32))).astype(BF16)
        y_ref[mine, :] = y_half

    def frows(d, c):
        return pl.ds(pl.multiple_of(d * B + c * HALF, HALF), HALF)

    with jax.named_scope('gather'):
        own = frows(dp, core)
        fall[own, :] = _rms(y_half.astype(F32), gain_f)
        gathers = [remote(fall.at[own], fall.at[own], 7 + i, dp=d) for i, d in enumerate((ydp, zdp, ddp))]
        for c in gathers:
            c.start()
        c6 = remote(fall.at[own], fall.at[own], 6, tp=sib)
        c6.start()
        c5 = remote(y_ref.at[mine], y_ref.at[mine], 5, tp=sib)
        c5.start()
        forwards = []
        for i, d in enumerate((ydp, zdp, ddp)):
            gathers[i].wait_recv()
            fwd = remote(fall.at[frows(d, core)], fall.at[frows(d, core)], 10 + i, tp=sib)
            fwd.start()
            forwards.append(fwd)
        for c in tok_copies:
            c.wait()
        lane = lax.broadcasted_iota(jnp.int32, (8, 128), 1)
        lo = jnp.where(lane < B, toks[0], toks[1])
        hi = jnp.where(lane < B, toks[2], toks[3])
        want = jnp.concatenate([lo, hi], axis=1) - (tp * VOC + v0)
        first = 8 * (dp // 3)
        want = jnp.where((want >= first) & (want < first + VQ), want, -1)
        for c in gathers:
            c.wait_send()
        for c in forwards + [c5, c6]:
            c.wait()
        y_out.start()
        for j in range(NVC):
            hcopy(j).wait()

    sub = lax.broadcasted_iota(jnp.int32, (VC // 8, 8, NDP * B), 0) * 8 + lax.broadcasted_iota(
        jnp.int32, (VC // 8, 8, NDP * B), 1)

    def vocab(j, carry):
        top, total, target = carry
        z = _dot(wh[pl.ds(pl.multiple_of(j * VC, VC), VC), :], fall[...], NT)
        drop_first = (first > 0) & (j == 0)
        drop_last = (first == 0) & (j == NVC - 1)
        z = jnp.concatenate([
            jnp.where(drop_first, -jnp.inf, z[:8]), z[8:VC - 8], jnp.where(drop_last, -jnp.inf, z[VC - 8:])], axis=0)
        z = z.reshape(VC // 8, 8, NDP * B)
        new_top = jnp.maximum(top, jnp.max(z, axis=0))
        total = total * jnp.exp(top - new_top) + jnp.sum(jnp.exp(z - new_top[None]), axis=0)
        hit = sub == (want - j * VC)[None]
        target = target + jnp.sum(jnp.where(hit, z, 0.0), axis=0)
        return new_top, total, target

    with jax.named_scope('head'):
        def several(i, carry):
            for k in range(UNROLL):
                carry = vocab(i * UNROLL + k, carry)
            return carry

        top, total, target = lax.fori_loop(0, NVC // UNROLL, several, (
            jnp.full((8, NDP * B), -jnp.inf, F32), jnp.zeros((8, NDP * B), F32), jnp.zeros((8, NDP * B), F32)))

    with jax.named_scope('stats'):
        t_row = jnp.max(top, axis=0, keepdims=True)
        s_row = jnp.sum(total * jnp.exp(top - t_row), axis=0, keepdims=True)
        z_row = jnp.sum(target, axis=0, keepdims=True)
        row8 = lax.broadcasted_iota(jnp.int32, (8, NDP * B), 0)
        stats = jnp.where(row8 == 0, t_row, jnp.where(row8 == 1, s_row, z_row))
        st_out[0] = stats[:, :128]
        st_out[1] = stats[:, 128:]
        st_in[me] = jnp.where(dp // 2 == 0, stats[:, :128], stats[:, 128:])
        st_copies = []
        for k in range(1, NDP * NTP):
            there = (me + k) % (NDP * NTP)
            c = pltpu.make_async_remote_copy(
                src_ref=st_out.at[there // NTP // 2], dst_ref=st_in.at[me], send_sem=st_send.at[k],
                recv_sem=st_recv.at[k], device_id={'dp': there // NTP, 'tp': there % NTP}, device_id_type=MESH)
            c.start()
            st_copies.append(c)
        for c in st_copies:
            c.wait()
        y_out.wait()


def finish_kernel(y_in, stats_h, y_ref, logp_ref, lse_ref, ybuf, stats_ref, sem):
    get_y = pltpu.make_async_copy(y_in, ybuf, sem.at[0])
    put_y = pltpu.make_async_copy(ybuf, y_ref, sem.at[1])
    get_stats = pltpu.make_async_copy(stats_h, stats_ref, sem.at[2])
    get_y.start()
    get_stats.start()
    get_y.wait()
    put_y.start()
    get_stats.wait()
    every = stats_ref[...]
    best = jnp.max(every[:, 0:1, :], axis=0)
    mass = jnp.sum(every[:, 1:2, :] * jnp.exp(every[:, 0:1, :] - best[None]), axis=0)
    hits = jnp.sum(every[:, 2:3, :], axis=0)
    lse = best + jnp.log(mass)
    logp = hits - lse
    left = lax.axis_index('dp') % 2 == 0
    lse_ref[...] = jnp.where(left, lse[:, :B], lse[:, B:])
    logp_ref[...] = jnp.where(left, logp[:, :B], logp[:, B:])
    put_y.wait()


def tail(part, x, g_mlp, g_final, next_tok, w_gate, w_up, w_down, w_head):
    vmem = pl.BlockSpec(memory_space=pltpu.VMEM)
    hbm = pl.BlockSpec(memory_space=pltpu.HBM)
    nff = len(FF_CHUNKS)
    half = pltpu.VMEM((HALF, D), BF16)
    y, stats = pl.pallas_call(
        tail_kernel,
        name='tail',
        out_shape=(
            jax.ShapeDtypeStruct((B, D), BF16),
            jax.ShapeDtypeStruct((NDP * NTP, 8, 128), F32),
        ),
        in_specs=[hbm] * 9,
        out_specs=(hbm, vmem),
        scratch_shapes=[
            pltpu.VMEM((B, D), BF16),
            pltpu.VMEM((B, D), BF16),
            pltpu.VMEM((D // 128, 128), BF16),
            pltpu.VMEM((D // 128, 128), BF16),
            pltpu.VMEM((1, B), jnp.int32),
            pltpu.VMEM((B, D), BF16),
            pltpu.VMEM((FF, D), BF16),
            pltpu.VMEM((FF, D), BF16),
            pltpu.VMEM((FF, D), BF16),
            pltpu.VMEM((VC * NVC, D), BF16),
            half, half, half,
            pltpu.VMEM((B, D), BF16),
            pltpu.VMEM((B, FF), BF16),
            pltpu.VMEM((B, D), BF16),
            half, half, half,
            pltpu.VMEM((NDP * B, D), BF16),
            pltpu.VMEM((NDP, 8, 128), jnp.int32),
            pltpu.VMEM((2, 8, 128), F32),
            pltpu.SemaphoreType.DMA((6,)),
            pltpu.SemaphoreType.DMA((nff,)),
            pltpu.SemaphoreType.DMA((nff,)),
            pltpu.SemaphoreType.DMA((1,)),
            pltpu.SemaphoreType.DMA((NVC,)),
            pltpu.SemaphoreType.DMA((16,)),
            pltpu.SemaphoreType.DMA((16,)),
            pltpu.SemaphoreType.DMA((16,)),
            pltpu.SemaphoreType.DMA((16,)),
        ],
        compiler_params=pltpu.CompilerParams(
            vmem_limit_bytes=61 * 1024 * 1024, collective_id=0, has_side_effects=True),
        cost_estimate=pl.CostEstimate(flops=10_000_000_000, bytes_accessed=50_000_000, transcendentals=0),
    )(part, x, g_mlp.reshape(D // 128, 128), g_final.reshape(D // 128, 128), next_tok.reshape(1, B),
      w_gate.T, w_up.T, w_down, w_head)
    return pl.pallas_call(
        finish_kernel,
        name='finish',
        out_shape=(
            jax.ShapeDtypeStruct((B, D), BF16),
            jax.ShapeDtypeStruct((1, B), F32),
            jax.ShapeDtypeStruct((1, B), F32),
        ),
        in_specs=[hbm] * 2,
        out_specs=(hbm, vmem, vmem),
        scratch_shapes=[
            pltpu.VMEM((B, D), BF16),
            pltpu.VMEM((NDP * NTP, 8, 128), F32),
            pltpu.SemaphoreType.DMA((3,)),
        ],
        compiler_params=pltpu.CompilerParams(vmem_limit_bytes=62 * 1024 * 1024),
    )(y, stats)


def local_step(tok_hidden, seq_lens, k_cache, v_cache, next_tok, g_attn, w_q, b_q, w_k, b_k, w_v, b_v, w_o, g_mlp,
               w_gate, w_up, w_down, g_final, w_head):
    part, k_all, v_all = attention(
        tok_hidden, seq_lens, k_cache.reshape(B, L, HD), v_cache.reshape(B, L, HD), g_attn, w_q, b_q, w_k, b_k, w_v,
        b_v, w_o)
    y_out, tok_logp, norm_lse = tail(part, tok_hidden, g_mlp, g_final, next_tok, w_gate, w_up, w_down, w_head)
    return (y_out, k_all.reshape(B, L, 1, HD), v_all.reshape(B, L, 1, HD), tok_logp.reshape(B), norm_lse.reshape(B))


def solution(mesh):
    row_spec = P('dp', None)
    vec_spec = P('dp')
    cache_spec = P('dp', None, 'tp', None)
    col_spec = P(None, 'tp')
    part_spec = P('tp')
    whole_spec = P(None)
    in_specs = (row_spec, vec_spec, cache_spec, cache_spec, vec_spec, whole_spec, col_spec, part_spec, col_spec,
                part_spec, col_spec, part_spec, P('tp', None), whole_spec, col_spec, col_spec, P('tp', None),
                whole_spec, P('tp', None))
    out_specs = (row_spec, cache_spec, cache_spec, vec_spec, vec_spec)
    return jax.shard_map(local_step, mesh=mesh, in_specs=in_specs, out_specs=out_specs, check_vma=False)
```

time: 80.6 us -> 61.3 us (0.76)
  local copies, waits for them, and re-layouts: 17.4 us -> 0 us
  Pallas kernels: 62.1 us -> 60.5 us
    unnamed x29 -> x0, local copies, waits for them, and re-layouts: 17.4 us -> none
    pallas_call x1, Pallas kernels: 50.1 us -> 43.8 us  [tail(): pl.pallas_call(tail_kernel, name='tail', out_shape=(jax.ShapeDtypeStruct(...]
    pallas_call x1, Pallas kernels: 11.9 us -> 14.6 us  [attention(): pl.pallas_call(attn_kernel, name='attn', out_shape=(jax.ShapeDtypeStruct(...]
    pallas_call x0 -> x1, Pallas kernels: none -> 2.14 us  [tail(): pl.pallas_call(finish_kernel, name='finish', out_shape=(jax.ShapeDtypeStr...]
where the time goes in v2:
time: 61.3 us; the launch traced here: 61.1 us
  Pallas kernels  60.5 us (99%)
  between operations  0.65 us (1%)
    pallas_call x1, Pallas kernels, tail(): pl.pallas_call(tail_kernel, name='tail', out_shape=(jax.ShapeDtypeStruct(...  43.8 us
    pallas_call x1, Pallas kernels, attention(): pl.pallas_call(attn_kernel, name='attn', out_shape=(jax.ShapeDtypeStruct(...  14.6 us
    pallas_call x1, Pallas kernels, tail(): pl.pallas_call(finish_kernel, name='finish', out_shape=(jax.ShapeDtypeStr...  2.14 us

profile of v2, /device:TPU:0, one launch (start us, length us, event | category | flops | bytes accessed | tf_op | source)
XLA Modules:
  0.0 61.1 jit_solution(9871303787766479797)
XLA Ops:
  0.6 14.6 %attn.1 = (bf16[64,1536]{1,0:T(8,128)(2,1)}, bf16[64,512,128]{2,1,0:T(8,128)(2,1)}, bf16[64,512,128]{2,1,0:T(8,128)(2,1)}) custom-call(bf16[64,1536]{1,0:T(8,128)(2,1)} %x_h.3, s32[1,64]{1,0:T(1,128)} %bitcast.28, bf16[12,128]{1,0:T(8,128)(2,1)} %bitcast.24, bf16[3,128]{1,0:T(4,128)(2,1)} %bitcast.27, bf16[1,128]{1,0:T(2,128)(2,1)} %bitcast.29, ...), custom_call_target="tpu_custom_call" | custom-call | flops 400000000 | bytes 37000000 | tf_op jit(solution)/shard_map/attn/pallas_call | solution.py:186
  15.2 43.8 %tail.1 = (bf16[64,1536]{1,0:T(8,128)(2,1)}, f32[16,8,128]{2,1,0:T(8,128)}) custom-call(bf16[64,1536]{1,0:T(8,128)(2,1)} %get-tuple-element.13.part_h, bf16[64,1536]{1,0:T(8,128)(2,1)} %x_h.3, bf16[12,128]{1,0:T(8,128)(2,1)} %bitcast.25, bf16[12,128]{1,0:T(8,128)(2,1)} %bitcast.26, s32[1,64]{1,0:T(1,128)} %bitcast.31, bf16[2240,1536]{1,0:T(8,128)(2,1)} %bitcast.22, ...), custom_call_target="tpu_custom_call" | custom-call | flops 10000000000 | bytes 50000000 | tf_op jit(solution)/shard_map/tail/pallas_call | solution.py:441
  59.0 2.1 %finish.1 = (bf16[64,1536]{1,0:T(8,128)(2,1)}, f32[1,64]{1,0:T(1,128)}, f32[1,64]{1,0:T(1,128)}) custom-call(bf16[64,1536]{1,0:T(8,128)(2,1)} %get-tuple-element.14.y_in, f32[16,8,128]{2,1,0:T(8,128)} %get-tuple-element.15.stats_h), custom_call_target="tpu_custom_call" | custom-call | tf_op jit(solution)/shard_map/finish/pallas_call | solution.py:484

commit v3 on v2

--- a/solution.py
+++ b/solution.py
@@ -40,6 +40,14 @@
     return lax.dot_general(a, b, dims, preferred_element_type=F32)
 
 
+def in_hbm(*arrays):
+    return [pltpu.with_memory_space_constraint(a, pltpu.HBM) for a in arrays]
+
+
+def in_vmem(*arrays):
+    return [pltpu.with_memory_space_constraint(a, pltpu.VMEM) for a in arrays]
+
+
 def _row(ref, n):
     vals = ref[...].astype(F32)
     return jnp.concatenate([vals[i:i + 1, :] for i in range(n)], axis=1)
@@ -50,13 +58,15 @@
     return (vals * inv * gain).astype(BF16)
 
 
-def attn_kernel(x_h, lens_h, g_h, bq_h, bk_h, bv_h, freq_h, wq_h, wk_h, wv_h, wo_h, k_h, v_h,
-                part_ref, ko_h, vo_h,
-                lens_s, x_ref, lens_ref, g_ref, bq_ref, bk_ref, bv_ref, freq_ref,
-                wq, wk, wv, wo, kbuf, vbuf, q_sc, kn_sc, vn_sc, len_sc, o_sc, isem, wsem, ksem, vsem, kosem, vosem):
+def attn_kernel(x_h, lens_h, g_h, bq_h, bk_h, bv_h, freq_h, gm_h, gf_h, tok_h, wq_h, wk_h, wv_h, wo_h, k_h, v_h,
+                part_ref, kbuf, vbuf, x_ref, gm_ref, gf_ref, tok_ref,
+                lens_s, lens_ref, g_ref, bq_ref, bk_ref, bv_ref, freq_ref,
+                wq, wk, wv, wo, q_sc, kn_sc, vn_sc, len_sc, o_sc, isem, wsem, ksem, vsem):
     small = [pltpu.make_async_copy(src, dst, isem.at[i]) for i, (src, dst) in enumerate((
         (x_h, x_ref), (g_h, g_ref), (lens_h, lens_ref), (freq_h, freq_ref), (bq_h, bq_ref), (bk_h, bk_ref),
         (bv_h, bv_ref), (lens_h, lens_s)))]
+    later = [pltpu.make_async_copy(src, dst, isem.at[8 + i]) for i, (src, dst) in enumerate((
+        (gm_h, gm_ref), (gf_h, gf_ref), (tok_h, tok_ref)))]
 
     def wcopy(i):
         src, dst = ((wq_h, wq), (wk_h, wk), (wv_h, wv), (wo_h, wo))[i]
@@ -70,18 +80,14 @@
 
     def vin(c):
         return pltpu.make_async_copy(v_h.at[rows(c)], vbuf.at[rows(c)], vsem.at[c])
-
-    def kout(c):
-        return pltpu.make_async_copy(kbuf.at[rows(c)], ko_h.at[rows(c)], kosem.at[c])
-
-    def vout(c):
-        return pltpu.make_async_copy(vbuf.at[rows(c)], vo_h.at[rows(c)], vosem.at[c])
 
     with jax.named_scope('starts'):
         for c in small:
             c.start()
         for i in range(3):
             wcopy(i).start()
+        for c in later:
+            c.start()
         for c in range(AHEAD):
             kin(c).start()
             vin(c).start()
@@ -159,8 +165,6 @@
             out = jnp.where(row_o == b, _dot(probs, vbuf[r0 + b], NN), out)
         for h in range(G):
             o_sc[pl.ds(r0, NB), h * HD:(h + 1) * HD] = out[h * NB:(h + 1) * NB, :]
-        kout(c).start()
-        vout(c).start()
         return carry
 
     with jax.named_scope('cache'):
@@ -168,17 +172,11 @@
     with jax.named_scope('proj'):
         wcopy(3).wait()
         part_ref[...] = _dot(o_sc[...].astype(BF16), wo[...], NN).astype(BF16)
-
-    def drain(c, carry):
-        kout(c).wait()
-        vout(c).wait()
-        return carry
-
-    with jax.named_scope('drain'):
-        lax.fori_loop(0, NCH, drain, 0)
-
-
-def attention(x, lens, k_cache, v_cache, g_attn, w_q, b_q, w_k, b_k, w_v, b_v, w_o):
+        for c in later:
+            c.wait()
+
+
+def attention(x, lens, k_cache, v_cache, g_attn, w_q, b_q, w_k, b_k, w_v, b_v, w_o, g_mlp, g_final, next_tok):
     inv_freq = np.power(THETA, np.arange(HD // 2, dtype=np.float64) * (-2.0 / HD)).astype(np.float32)
     freq = jnp.asarray(np.concatenate([inv_freq, inv_freq])[None, :])
     vmem = pl.BlockSpec(memory_space=pltpu.VMEM)
@@ -187,15 +185,13 @@
         attn_kernel,
         name='attn',
         out_shape=(
-            jax.ShapeDtypeStruct((B, D), BF16),
-            jax.ShapeDtypeStruct((B, L, HD), BF16),
-            jax.ShapeDtypeStruct((B, L, HD), BF16),
-        ),
-        in_specs=[hbm] * 13,
-        out_specs=(vmem, hbm, hbm),
+            pltpu.VMEM((B, D), BF16), pltpu.VMEM((B, L, HD), BF16), pltpu.VMEM((B, L, HD), BF16),
+            pltpu.VMEM((B, D), BF16), pltpu.VMEM((D // 128, 128), BF16), pltpu.VMEM((D // 128, 128), BF16),
+            pltpu.VMEM((1, B), jnp.int32)),
+        in_specs=[hbm] * 16,
+        out_specs=(vmem,) * 7,
         scratch_shapes=[
             pltpu.SMEM((1, B), jnp.int32),
-            pltpu.VMEM((B, D), BF16),
             pltpu.VMEM((1, B), jnp.int32),
             pltpu.VMEM((D // 128, 128), BF16),
             pltpu.VMEM((G, 128), BF16),
@@ -206,125 +202,169 @@
             pltpu.VMEM((D, HD), BF16),
             pltpu.VMEM((D, HD), BF16),
             pltpu.VMEM((G * HD, D), BF16),
-            pltpu.VMEM((B, L, HD), BF16),
-            pltpu.VMEM((B, L, HD), BF16),
             pltpu.VMEM((G, B, HD), F32),
             pltpu.VMEM((B, HD), F32),
             pltpu.VMEM((B, HD), F32),
             pltpu.VMEM((B, HD), F32),
             pltpu.VMEM((B, G * HD), F32),
-            pltpu.SemaphoreType.DMA((8,)),
+            pltpu.SemaphoreType.DMA((11,)),
             pltpu.SemaphoreType.DMA((4,)),
             pltpu.SemaphoreType.DMA((NCH,)),
             pltpu.SemaphoreType.DMA((NCH,)),
-            pltpu.SemaphoreType.DMA((NCH,)),
-            pltpu.SemaphoreType.DMA((NCH,)),
         ],
-        compiler_params=pltpu.CompilerParams(vmem_limit_bytes=62 * 1024 * 1024),
+        compiler_params=pltpu.CompilerParams(vmem_limit_bytes=8 * 1024 * 1024),
         cost_estimate=pl.CostEstimate(flops=400_000_000, bytes_accessed=37_000_000, transcendentals=0),
-    )(x, lens.reshape(1, B), g_attn.reshape(D // 128, 128), b_q.reshape(G, 128), b_k.reshape(1, 128),
-      b_v.reshape(1, 128), freq, w_q, w_k, w_v, w_o, k_cache, v_cache)
-
-
-def tail_kernel(part_h, x_h, gm_h, gf_h, tok_h, wg_h, wu_h, wd_h, wh_h,
-                y_h, st_in,
-                part_ref, x_ref, gm_ref, gf_ref, tok_ref, y_ref, wg, wu, wd, wh, r1, ps, r2, abuf, h_sc, dpart, r3, ps2, r4, fall, toks, st_out,
-                isem, gsem, usem, dsem, hsem, send, recv, st_send, st_recv):
-    dp = lax.axis_index('dp')
-    tp = lax.axis_index('tp')
-    core = tp % 2
-    sib = tp + 1 - 2 * core
-    xpeer = (tp + 2) % 4
-    me = dp * NTP + tp
-    ydp = dp + 1 - 2 * (dp % 2)
-    zdp = (dp + 2) % 4
-    ddp = (ydp + 2) % 4
-    mine = pl.ds(pl.multiple_of(core * HALF, HALF), HALF)
-    other = pl.ds(pl.multiple_of((1 - core) * HALF, HALF), HALF)
-
-    def gcopy(i):
-        s = pl.ds(*FF_CHUNKS[i])
-        return pltpu.make_async_copy(wg_h.at[s], wg.at[s], gsem.at[i])
-
-    def ucopy(i):
-        s = pl.ds(*FF_CHUNKS[i])
-        return pltpu.make_async_copy(wu_h.at[s], wu.at[s], usem.at[i])
-
-    dcopy = pltpu.make_async_copy(wd_h, wd, dsem.at[0])
-    v0 = dp * VQ - 8 * (dp // 3)
-
-    def hcopy(j):
-        src = wh_h.at[pl.ds(pl.multiple_of(v0 + j * VC, 8), VC)]
-        return pltpu.make_async_copy(src, wh.at[pl.ds(pl.multiple_of(j * VC, VC), VC)], hsem.at[j])
-
-    def remote(src, dst, i, **where):
+    )(*in_hbm(x, lens.reshape(1, B), g_attn.reshape(D // 128, 128), b_q.reshape(G, 128), b_k.reshape(1, 128),
+              b_v.reshape(1, 128), freq, g_mlp.reshape(D // 128, 128), g_final.reshape(D // 128, 128),
+              next_tok.reshape(1, B), w_q, w_k, w_v, w_o, k_cache, v_cache))
+
+
+class Place:
+    def __init__(self):
+        self.dp = lax.axis_index('dp')
+        self.tp = lax.axis_index('tp')
+        self.core = self.tp % 2
+        self.sib = self.tp + 1 - 2 * self.core
+        self.xpeer = (self.tp + 2) % 4
+        self.me = self.dp * NTP + self.tp
+        self.ydp = self.dp + 1 - 2 * (self.dp % 2)
+        self.zdp = (self.dp + 2) % 4
+        self.ddp = (self.ydp + 2) % 4
+        self.mine = pl.ds(pl.multiple_of(self.core * HALF, HALF), HALF)
+        self.other = pl.ds(pl.multiple_of((1 - self.core) * HALF, HALF), HALF)
+
+
+def _remote(send, recv):
+    def make(src, dst, i, **where):
         return pltpu.make_async_remote_copy(src_ref=src, dst_ref=dst, send_sem=send.at[i], recv_sem=recv.at[i],
                                             device_id=where, device_id_type=MESH)
-
-    small = [pltpu.make_async_copy(src, dst, isem.at[i]) for i, (src, dst) in enumerate((
-        (part_h, part_ref), (tok_h, tok_ref), (x_h, x_ref), (gm_h, gm_ref), (gf_h, gf_ref)))]
-    y_out = pltpu.make_async_copy(y_ref, y_h, isem.at[5])
+    return make
+
+
+def sum_kernel(part_ref, x_ref, wg_h, wu_h, wd_h, a_ref, wg, wu, wd, r1, ps, r2, wsem, send, recv):
+    at = Place()
+    mine = at.mine
+    remote = _remote(send, recv)
+    loads = [pltpu.make_async_copy(src, dst, wsem.at[i]) for i, (src, dst) in enumerate((
+        (wg_h, wg), (wu_h, wu), (wd_h, wd)))]
     barrier = pltpu.get_barrier_semaphore()
-    for k in range(1, NDP * NTP):
-        there = (me + k) % (NDP * NTP)
-        pl.semaphore_signal(barrier, inc=1, device_id={'dp': there // NTP, 'tp': there % NTP}, device_id_type=MESH)
-    for c in small:
+    pl.semaphore_signal(barrier, inc=1, device_id={'tp': at.sib}, device_id_type=MESH)
+    pl.semaphore_signal(barrier, inc=1, device_id={'tp': at.xpeer}, device_id_type=MESH)
+    for c in loads:
         c.start()
-    gcopy(0).start()
-    for c in small:
-        c.wait()
-    ucopy(0).start()
-    for i in range(1, len(FF_CHUNKS)):
-        gcopy(i).start()
-        ucopy(i).start()
-    dcopy.start()
-
-    tok2 = jnp.concatenate([tok_ref[...], tok_ref[...]], axis=1)
-    toks[dp] = jnp.broadcast_to(tok2, (8, 128))
-
-    with jax.named_scope('barrier'):
-        pl.semaphore_wait(barrier, NDP * NTP - 1)
-
+    with jax.named_scope('barrier1'):
+        pl.semaphore_wait(barrier, 2)
     with jax.named_scope('sum1'):
-        c0 = remote(part_ref.at[other], r1, 0, tp=sib)
+        c0 = remote(part_ref.at[at.other], r1, 0, tp=at.sib)
         c0.start()
-        tok_copies = [remote(toks.at[dp], toks.at[dp], 13 + i, dp=d) for i, d in enumerate((ydp, zdp, ddp))]
-        for c in tok_copies:
-            c.start()
         c0.wait()
         ps[...] = (part_ref[mine, :].astype(F32) + r1[...].astype(F32)).astype(BF16)
-        c1 = remote(ps, r2, 1, tp=xpeer)
+        c1 = remote(ps, r2, 1, tp=at.xpeer)
         c1.start()
-        gain_m = _row(gm_ref, D // 128)
-        gain_f = _row(gf_ref, D // 128)
         c1.wait()
-        a_half = (x_ref[mine, :].astype(F32) + (ps[...].astype(F32) + r2[...].astype(F32))).astype(BF16)
-        abuf[mine, :] = a_half
-        c2 = remote(abuf.at[mine], abuf.at[mine], 2, tp=sib)
+        a_ref[mine, :] = (x_ref[mine, :].astype(F32) + (ps[...].astype(F32) + r2[...].astype(F32))).astype(BF16)
+        c2 = remote(a_ref.at[mine], a_ref.at[mine], 2, tp=at.sib)
         c2.start()
         c2.wait()
-
+    with jax.named_scope('weights'):
+        for c in loads:
+            c.wait()
+
+
+def first_sum(part, x, w_gate, w_up, w_down):
+    vmem = pl.BlockSpec(memory_space=pltpu.VMEM)
+    hbm = pl.BlockSpec(memory_space=pltpu.HBM)
+    half = pltpu.VMEM((HALF, D), BF16)
+    weight = pltpu.VMEM((FF, D), BF16)
+    return pl.pallas_call(
+        sum_kernel,
+        name='first_sum',
+        out_shape=(pltpu.VMEM((B, D), BF16), weight, weight, weight),
+        in_specs=[vmem] * 2 + [hbm] * 3,
+        out_specs=(vmem,) * 4,
+        scratch_shapes=[
+            half, half, half,
+            pltpu.SemaphoreType.DMA((3,)),
+            pltpu.SemaphoreType.DMA((3,)),
+            pltpu.SemaphoreType.DMA((3,)),
+        ],
+        compiler_params=pltpu.CompilerParams(
+            vmem_limit_bytes=2 * 1024 * 1024, collective_id=1, has_side_effects=True),
+    )(*in_vmem(part, x), *in_hbm(w_gate.T, w_up.T, w_down))
+
+
+def mlp_kernel(a_ref, wg, wu, wd, kbuf, vbuf, gm_ref, dpart, ko_h, vo_h, h_sc, ksem, vsem):
+    puts = []
+    for c in range(NCH):
+        rows = pl.ds(c * NB, NB)
+        puts.append(pltpu.make_async_copy(kbuf.at[rows], ko_h.at[rows], ksem.at[c]))
+        puts.append(pltpu.make_async_copy(vbuf.at[rows], vo_h.at[rows], vsem.at[c]))
+    for c in puts:
+        c.start()
     with jax.named_scope('mlp'):
-        mlp_in = _rms(abuf[...].astype(F32), gain_m)
-        for i in range(len(FF_CHUNKS)):
-            gcopy(i).wait()
-            ucopy(i).wait()
-        dcopy.wait()
-        for j in range(NVC):
-            hcopy(j).start()
+        mlp_in = _rms(a_ref[...].astype(F32), _row(gm_ref, D // 128))
         for s, n in FF_CHUNKS:
             gate = _dot(mlp_in, wg[s:s + n, :], NT)
             up = _dot(mlp_in, wu[s:s + n, :], NT)
             h_sc[:, s:s + n] = (gate * (1.0 / (1.0 + jnp.exp(-gate))) * up).astype(BF16)
         dpart[...] = _dot(h_sc[...], wd[...], NN).astype(BF16)
+    with jax.named_scope('puts'):
+        for c in puts:
+            c.wait()
+
+
+def mlp(a, wg, wu, wd, k_new, v_new, g_mlp):
+    vmem = pl.BlockSpec(memory_space=pltpu.VMEM)
+    hbm = pl.BlockSpec(memory_space=pltpu.HBM)
+    cache = jax.ShapeDtypeStruct((B, L, HD), BF16)
+    return pl.pallas_call(
+        mlp_kernel,
+        name='mlp',
+        out_shape=(pltpu.VMEM((B, D), BF16), cache, cache),
+        in_specs=[vmem] * 7,
+        out_specs=(vmem, hbm, hbm),
+        scratch_shapes=[
+            pltpu.VMEM((B, FF), BF16),
+            pltpu.SemaphoreType.DMA((NCH,)),
+            pltpu.SemaphoreType.DMA((NCH,)),
+        ],
+        compiler_params=pltpu.CompilerParams(vmem_limit_bytes=8 * 1024 * 1024),
+    )(*in_vmem(a, wg, wu, wd, k_new, v_new, g_mlp))
+
+
+def tail_kernel(dpart, abuf, gf_ref, tok_ref, wh_h, y_ref, st_in,
+                wh, r3, ps2, r4, fall, toks, st_out, hsem, send, recv, st_send, st_recv):
+    at = Place()
+    dp, tp, me, mine = at.dp, at.tp, at.me, at.mine
+    remote = _remote(send, recv)
+    v0 = dp * VQ - 8 * (dp // 3)
+
+    def hcopy(j):
+        src = wh_h.at[pl.ds(pl.multiple_of(v0 + j * VC, 8), VC)]
+        return pltpu.make_async_copy(src, wh.at[pl.ds(pl.multiple_of(j * VC, VC), VC)], hsem.at[j])
+
+    barrier = pltpu.get_barrier_semaphore()
+    for k in range(1, NDP * NTP):
+        there = (me + k) % (NDP * NTP)
+        pl.semaphore_signal(barrier, inc=1, device_id={'dp': there // NTP, 'tp': there % NTP}, device_id_type=MESH)
+    for j in range(NVC):
+        hcopy(j).start()
+
+    with jax.named_scope('barrier'):
+        pl.semaphore_wait(barrier, NDP * NTP - 1)
 
     with jax.named_scope('sum2'):
-        c3 = remote(dpart.at[other], r3, 3, tp=sib)
+        c3 = remote(dpart.at[at.other], r3, 3, tp=at.sib)
         c3.start()
+        gain_f = _row(gf_ref, D // 128)
+        toks[dp] = jnp.broadcast_to(jnp.concatenate([tok_ref[...], tok_ref[...]], axis=1), (8, 128))
         c3.wait()
         ps2[...] = (dpart[mine, :].astype(F32) + r3[...].astype(F32)).astype(BF16)
-        c4 = remote(ps2, r4, 4, tp=xpeer)
+        c4 = remote(ps2, r4, 4, tp=at.xpeer)
         c4.start()
+        tok_copies = [remote(toks.at[dp], toks.at[dp], 13 + i, dp=d) for i, d in enumerate((at.ydp, at.zdp, at.ddp))]
+        for c in tok_copies:
+            c.start()
         c4.wait()
         y_half = (abuf[mine, :].astype(F32) + (ps2[...].astype(F32) + r4[...].astype(F32))).astype(BF16)
         y_ref[mine, :] = y_half
@@ -333,19 +373,19 @@
         return pl.ds(pl.multiple_of(d * B + c * HALF, HALF), HALF)
 
     with jax.named_scope('gather'):
-        own = frows(dp, core)
+        own = frows(dp, at.core)
         fall[own, :] = _rms(y_half.astype(F32), gain_f)
-        gathers = [remote(fall.at[own], fall.at[own], 7 + i, dp=d) for i, d in enumerate((ydp, zdp, ddp))]
+        gathers = [remote(fall.at[own], fall.at[own], 7 + i, dp=d) for i, d in enumerate((at.ydp, at.zdp, at.ddp))]
         for c in gathers:
             c.start()
-        c6 = remote(fall.at[own], fall.at[own], 6, tp=sib)
+        c6 = remote(fall.at[own], fall.at[own], 6, tp=at.sib)
         c6.start()
-        c5 = remote(y_ref.at[mine], y_ref.at[mine], 5, tp=sib)
+        c5 = remote(y_ref.at[mine], y_ref.at[mine], 5, tp=at.sib)
         c5.start()
         forwards = []
-        for i, d in enumerate((ydp, zdp, ddp)):
+        for i, d in enumerate((at.ydp, at.zdp, at.ddp)):
             gathers[i].wait_recv()
-            fwd = remote(fall.at[frows(d, core)], fall.at[frows(d, core)], 10 + i, tp=sib)
+            fwd = remote(fall.at[frows(d, at.core)], fall.at[frows(d, at.core)], 10 + i, tp=at.sib)
             fwd.start()
             forwards.append(fwd)
         for c in tok_copies:
@@ -360,7 +400,6 @@
             c.wait_send()
         for c in forwards + [c5, c6]:
             c.wait()
-        y_out.start()
         for j in range(NVC):
             hcopy(j).wait()
 
@@ -409,18 +448,11 @@
             st_copies.append(c)
         for c in st_copies:
             c.wait()
-        y_out.wait()
-
-
-def finish_kernel(y_in, stats_h, y_ref, logp_ref, lse_ref, ybuf, stats_ref, sem):
-    get_y = pltpu.make_async_copy(y_in, ybuf, sem.at[0])
-    put_y = pltpu.make_async_copy(ybuf, y_ref, sem.at[1])
-    get_stats = pltpu.make_async_copy(stats_h, stats_ref, sem.at[2])
-    get_y.start()
-    get_stats.start()
-    get_y.wait()
+
+
+def finish_kernel(ybuf, stats_ref, y_ref, logp_ref, lse_ref, sem):
+    put_y = pltpu.make_async_copy(ybuf, y_ref, sem.at[0])
     put_y.start()
-    get_stats.wait()
     every = stats_ref[...]
     best = jnp.max(every[:, 0:1, :], axis=0)
     mass = jnp.sum(every[:, 1:2, :] * jnp.exp(every[:, 0:1, :] - best[None]), axis=0)
@@ -433,43 +465,22 @@
     put_y.wait()
 
 
-def tail(part, x, g_mlp, g_final, next_tok, w_gate, w_up, w_down, w_head):
+def tail(dpart, a, g_final, next_tok, w_head):
     vmem = pl.BlockSpec(memory_space=pltpu.VMEM)
     hbm = pl.BlockSpec(memory_space=pltpu.HBM)
-    nff = len(FF_CHUNKS)
     half = pltpu.VMEM((HALF, D), BF16)
     y, stats = pl.pallas_call(
         tail_kernel,
         name='tail',
-        out_shape=(
-            jax.ShapeDtypeStruct((B, D), BF16),
-            jax.ShapeDtypeStruct((NDP * NTP, 8, 128), F32),
-        ),
-        in_specs=[hbm] * 9,
-        out_specs=(hbm, vmem),
+        out_shape=(pltpu.VMEM((B, D), BF16), pltpu.VMEM((NDP * NTP, 8, 128), F32)),
+        in_specs=[vmem] * 4 + [hbm],
+        out_specs=(vmem, vmem),
         scratch_shapes=[
-            pltpu.VMEM((B, D), BF16),
-            pltpu.VMEM((B, D), BF16),
-            pltpu.VMEM((D // 128, 128), BF16),
-            pltpu.VMEM((D // 128, 128), BF16),
-            pltpu.VMEM((1, B), jnp.int32),
-            pltpu.VMEM((B, D), BF16),
-            pltpu.VMEM((FF, D), BF16),
-            pltpu.VMEM((FF, D), BF16),
-            pltpu.VMEM((FF, D), BF16),
             pltpu.VMEM((VC * NVC, D), BF16),
-            half, half, half,
-            pltpu.VMEM((B, D), BF16),
-            pltpu.VMEM((B, FF), BF16),
-            pltpu.VMEM((B, D), BF16),
             half, half, half,
             pltpu.VMEM((NDP * B, D), BF16),
             pltpu.VMEM((NDP, 8, 128), jnp.int32),
             pltpu.VMEM((2, 8, 128), F32),
-            pltpu.SemaphoreType.DMA((6,)),
-            pltpu.SemaphoreType.DMA((nff,)),
-            pltpu.SemaphoreType.DMA((nff,)),
-            pltpu.SemaphoreType.DMA((1,)),
             pltpu.SemaphoreType.DMA((NVC,)),
             pltpu.SemaphoreType.DMA((16,)),
             pltpu.SemaphoreType.DMA((16,)),
@@ -477,10 +488,9 @@
             pltpu.SemaphoreType.DMA((16,)),
         ],
         compiler_params=pltpu.CompilerParams(
-            vmem_limit_bytes=61 * 1024 * 1024, collective_id=0, has_side_effects=True),
+            vmem_limit_bytes=56 * 1024 * 1024, collective_id=0, has_side_effects=True),
         cost_estimate=pl.CostEstimate(flops=10_000_000_000, bytes_accessed=50_000_000, transcendentals=0),
-    )(part, x, g_mlp.reshape(D // 128, 128), g_final.reshape(D // 128, 128), next_tok.reshape(1, B),
-      w_gate.T, w_up.T, w_down, w_head)
+    )(*in_vmem(dpart, a, g_final, next_tok), *in_hbm(w_head))
     return pl.pallas_call(
         finish_kernel,
         name='finish',
@@ -489,23 +499,21 @@
             jax.ShapeDtypeStruct((1, B), F32),
             jax.ShapeDtypeStruct((1, B), F32),
         ),
-        in_specs=[hbm] * 2,
+        in_specs=[vmem] * 2,
         out_specs=(hbm, vmem, vmem),
-        scratch_shapes=[
-            pltpu.VMEM((B, D), BF16),
-            pltpu.VMEM((NDP * NTP, 8, 128), F32),
-            pltpu.SemaphoreType.DMA((3,)),
-        ],
+        scratch_shapes=[pltpu.SemaphoreType.DMA((1,))],
         compiler_params=pltpu.CompilerParams(vmem_limit_bytes=62 * 1024 * 1024),
-    )(y, stats)
+    )(*in_vmem(y, stats))
 
 
 def local_step(tok_hidden, seq_lens, k_cache, v_cache, next_tok, g_attn, w_q, b_q, w_k, b_k, w_v, b_v, w_o, g_mlp,
                w_gate, w_up, w_down, g_final, w_head):
-    part, k_all, v_all = attention(
+    part, k_new, v_new, x, gm, gf, tok = attention(
         tok_hidden, seq_lens, k_cache.reshape(B, L, HD), v_cache.reshape(B, L, HD), g_attn, w_q, b_q, w_k, b_k, w_v,
-        b_v, w_o)
-    y_out, tok_logp, norm_lse = tail(part, tok_hidden, g_mlp, g_final, next_tok, w_gate, w_up, w_down, w_head)
+        b_v, w_o, g_mlp, g_final, next_tok)
+    a, wg, wu, wd = first_sum(part, x, w_gate, w_up, w_down)
+    dpart, k_all, v_all = mlp(a, wg, wu, wd, k_new, v_new, gm)
+    y_out, tok_logp, norm_lse = tail(dpart, a, gf, tok, w_head)
     return (y_out, k_all.reshape(B, L, 1, HD), v_all.reshape(B, L, 1, HD), tok_logp.reshape(B), norm_lse.reshape(B))
 
 

time: 61.3 us -> 62.2 us (1.015)
  Pallas kernels: 60.5 us -> 61.4 us
    pallas_call x2 -> x4, Pallas kernels: 58.3 us -> 60.2 us  [the longest x1 30.4 us: tail(): pl.pallas_call(tail_kernel, name='tail', out_shape=(pltpu.VMEM((B, D), BF...]
    pallas_call x1, Pallas kernels: 2.14 us -> 1.2 us  [tail(): pl.pallas_call(finish_kernel, name='finish', out_shape=(jax.ShapeDtypeStr...]
where the time goes in v3:
time: 62.2 us; the launch traced here: 62.1 us
  Pallas kernels  61.4 us (99%)
  between operations  0.67 us (1%)
    pallas_call x1, Pallas kernels, tail(): pl.pallas_call(tail_kernel, name='tail', out_shape=(pltpu.VMEM((B, D), BF...  30.4 us
    pallas_call x1, Pallas kernels, attention(): pl.pallas_call(attn_kernel, name='attn', out_shape=(pltpu.VMEM((B, D), BF...  12 us
    pallas_call x1, Pallas kernels, mlp(): pl.pallas_call(mlp_kernel, name='mlp', out_shape=(pltpu.VMEM((B, D), BF16...  9.04 us
    pallas_call x1, Pallas kernels, first_sum(): pl.pallas_call(sum_kernel, name='first_sum', out_shape=(pltpu.VMEM((B, D)...  8.75 us

profile of v3, /device:TPU:0, one launch (start us, length us, event | category | flops | bytes accessed | tf_op | source)
XLA Modules:
  0.0 62.1 jit_solution(7880056329561512949)
XLA Ops:
  0.6 12.0 %attn.1 = (bf16[64,1536]{1,0:T(8,128)(2,1)S(1)}, bf16[64,512,128]{2,1,0:T(8,128)(2,1)S(1)}, bf16[64,512,128]{2,1,0:T(8,128)(2,1)S(1)}, bf16[64,1536]{1,0:T(8,128...) custom-call(bf16[64,1536]{1,0:T(8,128)(2,1)} %x_h.1, s32[1,64]{1,0:T(1,128)} %bitcast.28, ...), custom_call_target="tpu_custom_call" | custom-call | flops 400000000 | bytes 37000000 | tf_op jit(solution)/shard_map/attn/pallas_call | solution.py:184
  12.6 8.8 %first_sum.1 = (bf16[64,1536]{1,0:T(8,128)(2,1)S(1)}, bf16[2240,1536]{1,0:T(8,128)(2,1)S(1)}, bf16[2240,1536]{1,0:T(8,128)(2,1)S(1)}, bf16[2240,1536]{1,0:T(8,128)(2,1)S(1)}) custom-call(bf16[64,1536]{1,0:T(8,128)(2,1)S(1)} %get-tuple-element.24.part_ref, bf16[64,1536]{1,0:T(8,128)(2,1)S(1)} %get-tuple-element.25.x_ref, bf16[2240,1536]{1,0:T(8,128)(2,1)} %bitcast.22, ...), custom_call_target="tpu_custom_call" | custom-call | tf_op jit(solution)/shard_map/first_sum/pallas_call | solution.py:279
  21.4 9.0 %mlp.1 = (bf16[64,1536]{1,0:T(8,128)(2,1)S(1)}, bf16[64,512,128]{2,1,0:T(8,128)(2,1)}, bf16[64,512,128]{2,1,0:T(8,128)(2,1)}) custom-call(bf16[64,1536]{1,0:T(8,128)(2,1)S(1)} %get-tuple-element.26.a_ref.abuf, bf16[2240,1536]{1,0:T(8,128)(2,1)S(1)} %get-tuple-element.27.wg, bf16[2240,1536]{1,0:T(8,128)(2,1)S(1)} %get-tuple-element.28.wu, ...), custom_call_target="tpu_custom_call" | custom-call | tf_op jit(solution)/shard_map/mlp/pallas_call | solution.py:320
  30.5 30.4 %tail.1 = (bf16[64,1536]{1,0:T(8,128)(2,1)S(1)}, f32[16,8,128]{2,1,0:T(8,128)S(1)}) custom-call(bf16[64,1536]{1,0:T(8,128)(2,1)S(1)} %get-tuple-element.33.dpart, bf16[64,1536]{1,0:T(8,128)(2,1)S(1)} %get-tuple-element.26.a_ref.abuf, bf16[12,128]{1,0:T(8,128)(2,1)S(1)} %get-tuple-element.34.gf_ref, s32[1,64]{1,0:T(1,128)S(1)} %get-tuple-element.35.tok_ref, ...), custom_call_target="tpu_custom_call" | custom-call | flops 10000000000 | bytes 50000000 | tf_op jit(solution)/shard_map/tail/pallas_call | solution.py:472
  60.9 1.2 %finish.1 = (bf16[64,1536]{1,0:T(8,128)(2,1)}, f32[1,64]{1,0:T(1,128)}, f32[1,64]{1,0:T(1,128)}) custom-call(bf16[64,1536]{1,0:T(8,128)(2,1)S(1)} %get-tuple-element.36.ybuf, f32[16,8,128]{2,1,0:T(8,128)S(1)} %get-tuple-element.37.stats_ref), custom_call_target="tpu_custom_call" | custom-call | tf_op jit(solution)/shard_map/finish/pallas_call | solution.py:494

commit v4 on v3

--- a/solution.py
+++ b/solution.py
@@ -23,13 +23,14 @@
 VOC = 37984
 NDP = 4
 NTP = 4
-NB = 8
+NB = 16
 NCH = B // NB
-AHEAD = 3
+AHEAD = 2
 VQ = VOC // NDP
 VC = 528
 NVC = 18
-UNROLL = 6
+UNROLL = 9
+KCUT = 512
 HALF = B // 2
 FF_CHUNKS = ((0, 512), (512, 512), (1024, 512), (1536, 512), (2048, 192))
 NT = (((1,), (1,)), ((), ()))
@@ -59,7 +60,7 @@
 
 
 def attn_kernel(x_h, lens_h, g_h, bq_h, bk_h, bv_h, freq_h, gm_h, gf_h, tok_h, wq_h, wk_h, wv_h, wo_h, k_h, v_h,
-                part_ref, kbuf, vbuf, x_ref, gm_ref, gf_ref, tok_ref,
+                part_ref, k0, k1, k2, k3, v0, v1, v2, v3, x_ref, gm_ref, gf_ref, tok_ref,
                 lens_s, lens_ref, g_ref, bq_ref, bk_ref, bv_ref, freq_ref,
                 wq, wk, wv, wo, q_sc, kn_sc, vn_sc, len_sc, o_sc, isem, wsem, ksem, vsem):
     small = [pltpu.make_async_copy(src, dst, isem.at[i]) for i, (src, dst) in enumerate((
@@ -72,14 +73,14 @@
         src, dst = ((wq_h, wq), (wk_h, wk), (wv_h, wv), (wo_h, wo))[i]
         return pltpu.make_async_copy(src, dst, wsem.at[i])
 
-    def rows(c):
-        return pl.ds(pl.multiple_of(c * NB, NB), NB)
+    kbufs = (k0, k1, k2, k3)
+    vbufs = (v0, v1, v2, v3)
 
     def kin(c):
-        return pltpu.make_async_copy(k_h.at[rows(c)], kbuf.at[rows(c)], ksem.at[c])
+        return pltpu.make_async_copy(k_h.at[pl.ds(c * NB, NB)], kbufs[c], ksem.at[c])
 
     def vin(c):
-        return pltpu.make_async_copy(v_h.at[rows(c)], vbuf.at[rows(c)], vsem.at[c])
+        return pltpu.make_async_copy(v_h.at[pl.ds(c * NB, NB)], vbufs[c], vsem.at[c])
 
     with jax.named_scope('starts'):
         for c in small:
@@ -121,54 +122,60 @@
         vn_sc[...] = (_dot(normed, wv[...], NN) + bv_ref[...].astype(F32)).astype(BF16).astype(F32)
 
     scale = HD ** -0.5
+    ncol = G * NB
     sub16 = lax.broadcasted_iota(jnp.int32, (16, HD), 0)
-    col_id = lax.broadcasted_iota(jnp.int32, (G * NB, L), 1).astype(F32)
-    row_s = lax.broadcasted_iota(jnp.int32, (G * NB, L), 0) % NB
-    row_o = lax.broadcasted_iota(jnp.int32, (G * NB, HD), 0) % NB
-
-    def chunk(c, carry):
-        r0 = pl.multiple_of(c * NB, NB)
-        kin(c).wait()
-        vin(c).wait()
-
-        @pl.when(c + AHEAD < NCH)
-        def _():
-            kin(c + AHEAD).start()
-            vin(c + AHEAD).start()
-
-        @pl.when(c + AHEAD == NCH)
-        def _():
-            wcopy(3).start()
-
+    col_id = lax.broadcasted_iota(jnp.int32, (ncol, L), 1).astype(F32)
+    row_q = lax.broadcasted_iota(jnp.int32, (ncol, NB * HD), 0) % NB
+    blk_q = lax.broadcasted_iota(jnp.int32, (ncol, NB * HD), 1) // HD
+    row_o = lax.broadcasted_iota(jnp.int32, (ncol, HD), 0) % NB
+
+    def fresh_rows(buf, new, c):
         for b in range(NB):
-            row = r0 + b
-            length = lens_s[0, row]
+            length = lens_s[0, c * NB + b]
             base = pl.multiple_of((length // 16) * 16, 16)
-            hit = sub16 == length - base
-            for buf, new in ((kbuf, kn_sc), (vbuf, vn_sc)):
-                old = buf[row, pl.ds(base, 16), :].astype(F32)
-                fresh = jnp.broadcast_to(new[pl.ds(row, 1), :], (16, HD))
-                buf[row, pl.ds(base, 16), :] = jnp.where(hit, fresh, old).astype(BF16)
-        q8 = jnp.concatenate([q_sc[h, pl.ds(r0, NB), :] for h in range(G)], axis=0).astype(BF16)
-        scores = jnp.zeros((G * NB, L), F32)
-        for b in range(NB):
-            scores = jnp.where(row_s == b, _dot(q8, kbuf[r0 + b], NT), scores)
-        len8 = len_sc[pl.ds(r0, NB), :]
-        len24 = jnp.concatenate([len8] * G, axis=0)
-        keep = col_id <= jnp.concatenate([len24] * (L // HD), axis=1)
+            old = buf[b, pl.ds(base, 16), :].astype(F32)
+            row = jnp.broadcast_to(new[c * NB + b:c * NB + b + 1, :], (16, HD))
+            buf[b, pl.ds(base, 16), :] = jnp.where(sub16 == length - base, row, old).astype(BF16)
+
+    def side(buf, first, count):
+        return jnp.concatenate([buf[first + b] for b in range(count)], axis=1)
+
+    def score(c):
+        heads = jnp.concatenate([q_sc[h, c * NB:(c + 1) * NB, :] for h in range(G)], axis=0)
+        wide = jnp.concatenate([heads] * NB, axis=1)
+        wide = jnp.where(row_q == blk_q, wide, 0.0).astype(BF16)
+        return _dot(wide, side(kbufs[c], 0, NB), NT)
+
+    def attend(c, scores):
+        last = jnp.concatenate([len_sc[c * NB:(c + 1) * NB, :]] * G, axis=0)
+        keep = col_id <= jnp.concatenate([last] * (L // HD), axis=1)
         scores = jnp.where(keep, scores * scale, -jnp.inf)
-        top = jnp.max(scores, axis=1, keepdims=True)
-        exps = jnp.exp(scores - top)
+        exps = jnp.exp(scores - jnp.max(scores, axis=1, keepdims=True))
         probs = (exps / jnp.sum(exps, axis=1, keepdims=True)).astype(BF16)
-        out = jnp.zeros((G * NB, HD), F32)
-        for b in range(NB):
-            out = jnp.where(row_o == b, _dot(probs, vbuf[r0 + b], NN), out)
+        out = jnp.zeros((ncol, HD), F32)
+        for b in range(0, NB, 2):
+            both = _dot(probs, side(vbufs[c], b, 2), NN)
+            out = jnp.where(row_o == b, both[:, :HD], jnp.where(row_o == b + 1, both[:, HD:], out))
         for h in range(G):
-            o_sc[pl.ds(r0, NB), h * HD:(h + 1) * HD] = out[h * NB:(h + 1) * NB, :]
-        return carry
+            o_sc[c * NB:(c + 1) * NB, h * HD:(h + 1) * HD] = out[h * NB:(h + 1) * NB, :]
 
     with jax.named_scope('cache'):
-        lax.fori_loop(0, NCH, chunk, 0)
+        scores = None
+        for c in range(NCH):
+            kin(c).wait()
+            vin(c).wait()
+            if c + AHEAD < NCH:
+                kin(c + AHEAD).start()
+                vin(c + AHEAD).start()
+            if c + AHEAD == NCH:
+                wcopy(3).start()
+            fresh_rows(kbufs[c], kn_sc, c)
+            fresh_rows(vbufs[c], vn_sc, c)
+            fresh_scores = score(c)
+            if c > 0:
+                attend(c - 1, scores)
+            scores = fresh_scores
+        attend(NCH - 1, scores)
     with jax.named_scope('proj'):
         wcopy(3).wait()
         part_ref[...] = _dot(o_sc[...].astype(BF16), wo[...], NN).astype(BF16)
@@ -185,11 +192,10 @@
         attn_kernel,
         name='attn',
         out_shape=(
-            pltpu.VMEM((B, D), BF16), pltpu.VMEM((B, L, HD), BF16), pltpu.VMEM((B, L, HD), BF16),
-            pltpu.VMEM((B, D), BF16), pltpu.VMEM((D // 128, 128), BF16), pltpu.VMEM((D // 128, 128), BF16),
-            pltpu.VMEM((1, B), jnp.int32)),
+            pltpu.VMEM((B, D), BF16), *[pltpu.VMEM((NB, L, HD), BF16)] * (2 * NCH), pltpu.VMEM((B, D), BF16),
+            pltpu.VMEM((D // 128, 128), BF16), pltpu.VMEM((D // 128, 128), BF16), pltpu.VMEM((1, B), jnp.int32)),
         in_specs=[hbm] * 16,
-        out_specs=(vmem,) * 7,
+        out_specs=(vmem,) * (5 + 2 * NCH),
         scratch_shapes=[
             pltpu.SMEM((1, B), jnp.int32),
             pltpu.VMEM((1, B), jnp.int32),
@@ -212,7 +218,7 @@
             pltpu.SemaphoreType.DMA((NCH,)),
             pltpu.SemaphoreType.DMA((NCH,)),
         ],
-        compiler_params=pltpu.CompilerParams(vmem_limit_bytes=8 * 1024 * 1024),
+        compiler_params=pltpu.CompilerParams(vmem_limit_bytes=16 * 1024 * 1024),
         cost_estimate=pl.CostEstimate(flops=400_000_000, bytes_accessed=37_000_000, transcendentals=0),
     )(*in_hbm(x, lens.reshape(1, B), g_attn.reshape(D // 128, 128), b_q.reshape(G, 128), b_k.reshape(1, 128),
               b_v.reshape(1, 128), freq, g_mlp.reshape(D // 128, 128), g_final.reshape(D // 128, 128),
@@ -293,14 +299,25 @@
     )(*in_vmem(part, x), *in_hbm(w_gate.T, w_up.T, w_down))
 
 
-def mlp_kernel(a_ref, wg, wu, wd, kbuf, vbuf, gm_ref, dpart, ko_h, vo_h, h_sc, ksem, vsem):
+def mlp_kernel(a_ref, wg, wu, wd, gm_ref, k0, k1, k2, k3, v0, v1, v2, v3, dpart, ko_h, vo_h, h_sc, ksem, vsem):
     puts = []
-    for c in range(NCH):
+    for c, (k, v) in enumerate(((k0, v0), (k1, v1), (k2, v2), (k3, v3))):
         rows = pl.ds(c * NB, NB)
-        puts.append(pltpu.make_async_copy(kbuf.at[rows], ko_h.at[rows], ksem.at[c]))
-        puts.append(pltpu.make_async_copy(vbuf.at[rows], vo_h.at[rows], vsem.at[c]))
-    for c in puts:
-        c.start()
+        puts.append(pltpu.make_async_copy(k, ko_h.at[rows], ksem.at[c]))
+        puts.append(pltpu.make_async_copy(v, vo_h.at[rows], vsem.at[c]))
+
+    def start(_, carry):
+        for c in puts:
+            c.start()
+        return carry
+
+    def finish(_, carry):
+        for c in puts:
+            c.wait()
+        return carry
+
+    once = lax.axis_index('tp') // NTP + 1
+    lax.fori_loop(0, once, start, 0)
     with jax.named_scope('mlp'):
         mlp_in = _rms(a_ref[...].astype(F32), _row(gm_ref, D // 128))
         for s, n in FF_CHUNKS:
@@ -309,11 +326,10 @@
             h_sc[:, s:s + n] = (gate * (1.0 / (1.0 + jnp.exp(-gate))) * up).astype(BF16)
         dpart[...] = _dot(h_sc[...], wd[...], NN).astype(BF16)
     with jax.named_scope('puts'):
-        for c in puts:
-            c.wait()
-
-
-def mlp(a, wg, wu, wd, k_new, v_new, g_mlp):
+        lax.fori_loop(0, once, finish, 0)
+
+
+def mlp(a, wg, wu, wd, g_mlp, caches):
     vmem = pl.BlockSpec(memory_space=pltpu.VMEM)
     hbm = pl.BlockSpec(memory_space=pltpu.HBM)
     cache = jax.ShapeDtypeStruct((B, L, HD), BF16)
@@ -321,7 +337,7 @@
         mlp_kernel,
         name='mlp',
         out_shape=(pltpu.VMEM((B, D), BF16), cache, cache),
-        in_specs=[vmem] * 7,
+        in_specs=[vmem] * (5 + 2 * NCH),
         out_specs=(vmem, hbm, hbm),
         scratch_shapes=[
             pltpu.VMEM((B, FF), BF16),
@@ -329,11 +345,11 @@
             pltpu.SemaphoreType.DMA((NCH,)),
         ],
         compiler_params=pltpu.CompilerParams(vmem_limit_bytes=8 * 1024 * 1024),
-    )(*in_vmem(a, wg, wu, wd, k_new, v_new, g_mlp))
+    )(*in_vmem(a, wg, wu, wd, g_mlp, *caches))
 
 
 def tail_kernel(dpart, abuf, gf_ref, tok_ref, wh_h, y_ref, st_in,
-                wh, r3, ps2, r4, fall, toks, st_out, hsem, send, recv, st_send, st_recv):
+                wh, r3, ps2, r4, f0, f1, zbuf, toks, st_out, hsem, send, recv, st_send, st_recv):
     at = Place()
     dp, tp, me, mine = at.dp, at.tp, at.me, at.mine
     remote = _remote(send, recv)
@@ -362,7 +378,7 @@
         ps2[...] = (dpart[mine, :].astype(F32) + r3[...].astype(F32)).astype(BF16)
         c4 = remote(ps2, r4, 4, tp=at.xpeer)
         c4.start()
-        tok_copies = [remote(toks.at[dp], toks.at[dp], 13 + i, dp=d) for i, d in enumerate((at.ydp, at.zdp, at.ddp))]
+        tok_copies = [remote(toks.at[dp], toks.at[dp], 19 + i, dp=d) for i, d in enumerate((at.ydp, at.zdp, at.ddp))]
         for c in tok_copies:
             c.start()
         c4.wait()
@@ -374,20 +390,21 @@
 
     with jax.named_scope('gather'):
         own = frows(dp, at.core)
-        fall[own, :] = _rms(y_half.astype(F32), gain_f)
-        gathers = [remote(fall.at[own], fall.at[own], 7 + i, dp=d) for i, d in enumerate((at.ydp, at.zdp, at.ddp))]
-        for c in gathers:
+        f_half = _rms(y_half.astype(F32), gain_f)
+        f0[own, :] = f_half[:, :KCUT]
+        f1[own, :] = f_half[:, KCUT:]
+        peers = (at.ydp, at.zdp, at.ddp)
+        gathers = [[remote(f.at[own], f.at[own], 7 + 3 * k + i, dp=d) for i, d in enumerate(peers)]
+                   for k, f in enumerate((f0, f1))]
+        passes = [[remote(f.at[frows(d, at.core)], f.at[frows(d, at.core)], 13 + 3 * k + i, tp=at.sib)
+                   for i, d in enumerate(peers)] for k, f in enumerate((f0, f1))]
+        keeps = [remote(f.at[own], f.at[own], 5 + k, tp=at.sib) for k, f in enumerate((f0, f1))]
+        c5 = remote(y_ref.at[mine], y_ref.at[mine], 2, tp=at.sib)
+        for c in gathers[0] + [keeps[0]] + gathers[1] + [keeps[1], c5]:
             c.start()
-        c6 = remote(fall.at[own], fall.at[own], 6, tp=at.sib)
-        c6.start()
-        c5 = remote(y_ref.at[mine], y_ref.at[mine], 5, tp=at.sib)
-        c5.start()
-        forwards = []
-        for i, d in enumerate((at.ydp, at.zdp, at.ddp)):
-            gathers[i].wait_recv()
-            fwd = remote(fall.at[frows(d, at.core)], fall.at[frows(d, at.core)], 10 + i, tp=at.sib)
-            fwd.start()
-            forwards.append(fwd)
+        for i in range(3):
+            gathers[0][i].wait_recv()
+            passes[0][i].start()
         for c in tok_copies:
             c.wait()
         lane = lax.broadcasted_iota(jnp.int32, (8, 128), 1)
@@ -396,19 +413,18 @@
         want = jnp.concatenate([lo, hi], axis=1) - (tp * VOC + v0)
         first = 8 * (dp // 3)
         want = jnp.where((want >= first) & (want < first + VQ), want, -1)
-        for c in gathers:
-            c.wait_send()
-        for c in forwards + [c5, c6]:
-            c.wait()
         for j in range(NVC):
             hcopy(j).wait()
+        for c in passes[0] + [keeps[0]]:
+            c.wait_recv()
 
     sub = lax.broadcasted_iota(jnp.int32, (VC // 8, 8, NDP * B), 0) * 8 + lax.broadcasted_iota(
         jnp.int32, (VC // 8, 8, NDP * B), 1)
 
     def vocab(j, carry):
         top, total, target = carry
-        z = _dot(wh[pl.ds(pl.multiple_of(j * VC, VC), VC), :], fall[...], NT)
+        part = pl.ds(pl.multiple_of(j * VC, VC), VC)
+        z = zbuf[part, :] + _dot(wh[part, KCUT:], f1[...], NT)
         drop_first = (first > 0) & (j == 0)
         drop_last = (first == 0) & (j == NVC - 1)
         z = jnp.concatenate([
@@ -420,6 +436,22 @@
         target = target + jnp.sum(jnp.where(hit, z, 0.0), axis=0)
         return new_top, total, target
 
+    def first_part(js):
+        for j in js:
+            part = pl.ds(j * VC, VC)
+            zbuf[part, :] = _dot(wh[part, :KCUT], f0[...], NT)
+
+    with jax.named_scope('head1'):
+        first_part(range(0, 6))
+        for i in range(2):
+            gathers[1][i].wait_recv()
+            passes[1][i].start()
+        first_part(range(6, 12))
+        gathers[1][2].wait_recv()
+        passes[1][2].start()
+        first_part(range(12, NVC))
+        for c in passes[1] + [keeps[1], c5]:
+            c.wait_recv()
     with jax.named_scope('head'):
         def several(i, carry):
             for k in range(UNROLL):
@@ -446,6 +478,8 @@
                 recv_sem=st_recv.at[k], device_id={'dp': there // NTP, 'tp': there % NTP}, device_id_type=MESH)
             c.start()
             st_copies.append(c)
+        for c in gathers[0] + gathers[1] + passes[0] + passes[1] + keeps + [c5]:
+            c.wait_send()
         for c in st_copies:
             c.wait()
 
@@ -478,12 +512,14 @@
         scratch_shapes=[
             pltpu.VMEM((VC * NVC, D), BF16),
             half, half, half,
-            pltpu.VMEM((NDP * B, D), BF16),
+            pltpu.VMEM((NDP * B, KCUT), BF16),
+            pltpu.VMEM((NDP * B, D - KCUT), BF16),
+            pltpu.VMEM((NVC * VC, NDP * B), F32),
             pltpu.VMEM((NDP, 8, 128), jnp.int32),
             pltpu.VMEM((2, 8, 128), F32),
             pltpu.SemaphoreType.DMA((NVC,)),
-            pltpu.SemaphoreType.DMA((16,)),
-            pltpu.SemaphoreType.DMA((16,)),
+            pltpu.SemaphoreType.DMA((22,)),
+            pltpu.SemaphoreType.DMA((22,)),
             pltpu.SemaphoreType.DMA((16,)),
             pltpu.SemaphoreType.DMA((16,)),
         ],
@@ -508,11 +544,11 @@
 
 def local_step(tok_hidden, seq_lens, k_cache, v_cache, next_tok, g_attn, w_q, b_q, w_k, b_k, w_v, b_v, w_o, g_mlp,
                w_gate, w_up, w_down, g_final, w_head):
-    part, k_new, v_new, x, gm, gf, tok = attention(
+    part, *caches, x, gm, gf, tok = attention(
         tok_hidden, seq_lens, k_cache.reshape(B, L, HD), v_cache.reshape(B, L, HD), g_attn, w_q, b_q, w_k, b_k, w_v,
         b_v, w_o, g_mlp, g_final, next_tok)
     a, wg, wu, wd = first_sum(part, x, w_gate, w_up, w_down)
-    dpart, k_all, v_all = mlp(a, wg, wu, wd, k_new, v_new, gm)
+    dpart, k_all, v_all = mlp(a, wg, wu, wd, gm, caches)
     y_out, tok_logp, norm_lse = tail(dpart, a, gf, tok, w_head)
     return (y_out, k_all.reshape(B, L, 1, HD), v_all.reshape(B, L, 1, HD), tok_logp.reshape(B), norm_lse.reshape(B))
 

time: 62.2 us -> 54.8 us (0.88)
  Pallas kernels: 61.4 us -> 53.9 us
    pallas_call x1, Pallas kernels: 9.04 us -> 5.94 us  [mlp(): pl.pallas_call(mlp_kernel, name='mlp', out_shape=(pltpu.VMEM((B, D), BF16...]
    pallas_call x1, Pallas kernels: 12 us -> 9.1 us  [attention(): pl.pallas_call(attn_kernel, name='attn', out_shape=(pltpu.VMEM((B, D), BF...]
    pallas_call x1, Pallas kernels: 30.4 us -> 28.9 us  [tail(): pl.pallas_call(tail_kernel, name='tail', out_shape=(pltpu.VMEM((B, D), BF...]
where the time goes in v4:
time: 54.8 us; the launch traced here: 54.7 us
  Pallas kernels  53.9 us (98%)
  between operations  0.83 us (2%)
    pallas_call x1, Pallas kernels, tail(): pl.pallas_call(tail_kernel, name='tail', out_shape=(pltpu.VMEM((B, D), BF...  28.9 us
    pallas_call x1, Pallas kernels, attention(): pl.pallas_call(attn_kernel, name='attn', out_shape=(pltpu.VMEM((B, D), BF...  9.1 us
    pallas_call x1, Pallas kernels, first_sum(): pl.pallas_call(sum_kernel, name='first_sum', out_shape=(pltpu.VMEM((B, D)...  8.75 us
    pallas_call x1, Pallas kernels, mlp(): pl.pallas_call(mlp_kernel, name='mlp', out_shape=(pltpu.VMEM((B, D), BF16...  5.94 us
    pallas_call x1, Pallas kernels, tail(): pl.pallas_call(finish_kernel, name='finish', out_shape=(jax.ShapeDtypeStr...  1.2 us

profile of v4, /device:TPU:0, one launch (start us, length us, event | category | flops | bytes accessed | tf_op | source)
XLA Modules:
  0.0 54.7 jit_solution(10824986984246258323)
XLA Ops:
  0.6 9.1 %attn.1 = (bf16[64,1536]{1,0:T(8,128)(2,1)S(1)}, bf16[16,512,128]{2,1,0:T(8,128)(2,1)S(1)}, bf16[16,512,128]{2,1,0:T(8,128)(2,1)S(1)}, bf16[16,512,128]{2,1,0:T(...) custom-call(bf16[64,1536]{1,0:T(8,128)(2,1)} %x_h.1, ...), custom_call_target="tpu_custom_call" | custom-call | flops 400000000 | bytes 37000000 | tf_op jit(solution)/shard_map/attn/pallas_call | solution.py:191
  9.7 8.8 %first_sum.1 = (bf16[64,1536]{1,0:T(8,128)(2,1)S(1)}, bf16[2240,1536]{1,0:T(8,128)(2,1)S(1)}, bf16[2240,1536]{1,0:T(8,128)(2,1)S(1)}, bf16[2240,1536]{1,0:T(8,128)(2,1)S(1)}) custom-call(bf16[64,1536]{1,0:T(8,128)(2,1)S(1)} %get-tuple-element.30.part_ref, bf16[64,1536]{1,0:T(8,128)(2,1)S(1)} %get-tuple-element.31.x_ref, bf16[2240,1536]{1,0:T(8,128)(2,1)} %bitcast.22, ...), custom_call_target="tpu_custom_call" | custom-call | tf_op jit(solution)/shard_map/first_sum/pallas_call | solution.py:285
  18.5 5.9 %mlp.1 = (bf16[64,1536]{1,0:T(8,128)(2,1)S(1)}, bf16[64,512,128]{2,1,0:T(8,128)(2,1)}, bf16[64,512,128]{2,1,0:T(8,128)(2,1)}) custom-call(bf16[64,1536]{1,0:T(8,128)(2,1)S(1)} %get-tuple-element.32.a_ref.abuf, bf16[2240,1536]{1,0:T(8,128)(2,1)S(1)} %get-tuple-element.33.wg, bf16[2240,1536]{1,0:T(8,128)(2,1)S(1)} %get-tuple-element.34.wu, ...), custom_call_target="tpu_custom_call" | custom-call | tf_op jit(solution)/shard_map/mlp/pallas_call | solution.py:336
  24.5 28.9 %tail.1 = (bf16[64,1536]{1,0:T(8,128)(2,1)S(1)}, f32[16,8,128]{2,1,0:T(8,128)S(1)}) custom-call(bf16[64,1536]{1,0:T(8,128)(2,1)S(1)} %get-tuple-element.45.dpart, bf16[64,1536]{1,0:T(8,128)(2,1)S(1)} %get-tuple-element.32.a_ref.abuf, bf16[12,128]{1,0:T(8,128)(2,1)S(1)} %get-tuple-element.46.gf_ref, s32[1,64]{1,0:T(1,128)S(1)} %get-tuple-element.47.tok_ref, ...), custom_call_target="tpu_custom_call" | custom-call | flops 10000000000 | bytes 50000000 | tf_op jit(solution)/shard_map/tail/pallas_call | solution.py:506
  53.3 1.2 %finish.1 = (bf16[64,1536]{1,0:T(8,128)(2,1)}, f32[1,64]{1,0:T(1,128)}, f32[1,64]{1,0:T(1,128)}) custom-call(bf16[64,1536]{1,0:T(8,128)(2,1)S(1)} %get-tuple-element.48.ybuf, f32[16,8,128]{2,1,0:T(8,128)S(1)} %get-tuple-element.49.stats_ref), custom_call_target="tpu_custom_call" | custom-call | tf_op jit(solution)/shard_map/finish/pallas_call | solution.py:530
